TPU v7x, 256 devices: a whole 4x4x8 slice. The times are simulated.
256 devices in a mesh: group: 4 (over y), dp: 8 (over z_lo, core), mp: 8 (over z_hi, x).
Axes of the slice: x: 4, y: 4, z: 8 (z_hi: 2, z_lo: 4; z = z_hi * 4 + z_lo), core: 2. Of those that a mesh axis runs over, the one named last changes fastest.
Arguments:
- patches: bfloat16 [1024, 12800], P(('group', 'mp'), 'dp'), may hold values from -6 to 6
- norm_gain: float32 [12800], P('dp'), may hold values from 0.25 to 1.75
- norm_bias: float32 [12800], P('dp'), may hold values from -3 to 3
- proj_in: bfloat16 [12800, 4096], P('dp', ('group', 'mp')), may hold values from -0.0546875 to 0.0546875
- proj_in_bias: float32 [4096], P(('group', 'mp')), may hold values from -3 to 3
- proj_out: bfloat16 [4096, 4096], P(('group', 'mp'), 'dp'), may hold values from -0.09375 to 0.09375
- proj_out_bias: float32 [4096], P('dp'), may hold values from -3 to 3
- text_rows: bfloat16 [1024, 4096], P(('group', 'mp'), 'dp'), may hold values from -6 to 6
- out_grads: bfloat16 [1024, 4096], P(('group', 'mp'), 'dp'), may hold values from -6 to 6
- gate_weight: bfloat16 [4096, 14336], P('dp', 'mp'), may hold values from -0.09375 to 0.09375
- up_weight: bfloat16 [4096, 14336], P('dp', 'mp'), may hold values from -0.09375 to 0.09375
- down_weight: bfloat16 [14336, 4096], P('mp', 'dp'), may hold values from -0.046875 to 0.046875
- image_counts: int32 [16], replicated, may hold values from 16 to 64, as said below
- image_sequence: int32 [16], replicated, may hold values from 0 to 7, as said below
- image_offsets: int32 [16], replicated, may hold values from 0 to 112, as said below
Outputs:
- projected: bfloat16 [1024, 4096], P(('group', 'mp'), 'dp')
- sequence_grads: bfloat16 [1024, 4096], P(('group', 'mp'), 'dp')
- row_grads: bfloat16 [1024, 4096], P(('group', 'mp'), 'dp')
Inputs may be any that keep to these rules, and one draw needn't show every extreme that they name: `image_counts`: image rows lie end to end from row 0 in image order; rows after the last image belong to no image. `image_sequence`: every sequence holds exactly two images. `image_offsets`: the two images of a sequence do not intersect and lie within its 128 rows.
All inputs are finite; a program needn't handle non-finite values.
Results may differ from a plain program's by a relative error of at most 0.0075.
Values may be sent and summed in bfloat16 or wider, within the bound.
No kernel may reach another device: no remote copies, remote signals or barrier semaphores. Data moves between devices by JAX's collectives and lax.ppermute only.
A program may use at most 64 MiB of HBM per device.

v0:
```python
import jax
import jax.numpy as jnp
from jax import lax
from jax.experimental import pallas as pl
from jax.experimental.pallas import tpu as pltpu
from jax.sharding import Mesh
from jax.sharding import PartitionSpec as P


TOK_DEV = 128
ROWS = ("g", "zh", "x")
DP = ("zl", "c")
MP = ("zh", "x")
BF = jnp.bfloat16
F32 = jnp.float32


def from_next(value, axis, k):
    n = lax.axis_size(axis)
    return lax.ppermute(value, axis, [((i + k) % n, i) for i in range(n)])


def swap(value, axis):
    return lax.ppermute(value, axis, [(0, 1), (1, 0)])


def copy_for_each(shard, axis):
    count = lax.axis_size(axis)
    return lax.all_to_all(
        jnp.broadcast_to(shard[None], (count, *shard.shape)), axis, 0, 0, tiled=True
    )


def in_order(own, other, index, dim=0):
    return jnp.where(
        index == 0,
        jnp.concatenate([own, other], axis=dim),
        jnp.concatenate([other, own], axis=dim),
    )


def line_of(value, axis):
    return [value] + [from_next(value, axis, k) for k in (1, 2, 3)]


def mm(a, b):
    return jnp.dot(a, b, preferred_element_type=F32)


def mm_t(a, b):
    return lax.dot_general(a, b, (((1,), (1,)), ((), ())), preferred_element_type=F32)


def pick(onehot, rows):
    return mm(onehot, rows).astype(BF)


def three_parts(v):
    hi = lax.reduce_precision(v, 8, 7)
    mid = lax.reduce_precision(v - hi, 8, 7)
    low = v - hi - mid
    return jnp.stack([hi, mid, low]).astype(BF)


def seq_sources(counts, sequence, offsets, rows):
    starts = jnp.cumsum(counts) - counts
    seq = rows // TOK_DEV
    pos = rows % TOK_DEV
    hit = (
        (sequence[None, :] == seq[:, None])
        & (offsets[None, :] <= pos[:, None])
        & (pos[:, None] < (offsets + counts)[None, :])
    )
    covered = jnp.any(hit, axis=1)
    source = lax.optimization_barrier(
        jnp.sum(jnp.where(hit, starts[None, :] + pos[:, None] - offsets[None, :], 0), axis=1)
    )
    return (source, covered)


def image_targets(counts, sequence, offsets, rows):
    starts = jnp.cumsum(counts) - counts
    hit = (starts[None, :] <= rows[:, None]) & (rows[:, None] < (starts + counts)[None, :])
    target = jnp.sum(
        jnp.where(
            hit, sequence[None, :] * TOK_DEV + offsets[None, :] + rows[:, None] - starts[None, :], 0
        ),
        axis=1,
    )
    return (target, jnp.any(hit, axis=1))


def unit_grads(gate, up, hidden_grad):
    sig = jax.nn.sigmoid(gate)
    gate_grad = (hidden_grad * up * sig * (1.0 + gate * (1.0 - sig))).astype(BF)
    up_grad = (hidden_grad * gate * sig).astype(BF)
    return (gate_grad, up_grad)


def row_share(kept, given, own):
    there = swap(given, "c")
    near = kept + there
    sent = near[own:].astype(BF)
    total = near[:own]
    for k in (1, 2, 3):
        total = total + from_next(sent[own * (3 - k) : own * (4 - k)], "zl", k).astype(F32)
    return total


VMEM = pl.BlockSpec(memory_space=pltpu.VMEM)
SMEM = pl.BlockSpec(memory_space=pltpu.SMEM)
ANY = pl.BlockSpec(memory_space=pl.ANY)


def first_kernel(
    c_ref, x0, x1, x2, x3, gain_ref, bias_ref, w0, w1, w2, w3,
    keep_ref, send_ref, out_ref, shift_ref, z_ref, w_ref, extra_ref, sems
):
    n, feats = x0.shape
    count = 4 * n
    units = w0.shape[1]
    half = 2 * units
    copies = []

    def copy(src, dst):
        copies.append(pltpu.make_async_copy(src, dst, sems.at[len(copies)]))
        copies[-1].start()

    ws = (w0, w1, w2, w3)
    for k, w in enumerate(ws):
        copy(w.at[pl.ds(0, feats)], w_ref.at[:, pl.ds(k * units, units)])
    for k, w in enumerate(ws):
        for j in range(out_ref.shape[1] // units):
            copy(
                w.at[pl.ds(feats + j * units, units)],
                out_ref.at[pl.ds(k * units, units), pl.ds(j * units, units)],
            )
        copy(w.at[pl.ds(w.shape[0] - 16, 16)], extra_ref.at[:, pl.ds(k * units, units)])
    gain = gain_ref[...]
    step = 16
    lane = lax.broadcasted_iota(jnp.int32, (step, units), 1)
    for k, x_ref in enumerate((x0, x1, x2, x3)):

        @pl.loop(0, n // step)
        def _(i):
            x = x_ref[pl.ds(pl.multiple_of(i * step, step), step), :].astype(F32)
            mean = jnp.sum(x, axis=1, keepdims=True) * (1.0 / feats)
            centred = x - mean
            spread = jnp.sum(centred * centred, axis=1, keepdims=True) * (1.0 / feats)
            rows = pl.ds(pl.multiple_of(k * n + i * step, step), step)
            z_ref[rows, :] = (centred * gain).astype(BF)
            stats = jnp.where(lane == 0, mean, jnp.where(lane == 1, spread, 0.0))
            for ref in (keep_ref, send_ref):
                ref[rows, half:] = stats

    extra = []
    for v in (gain, bias_ref[...]):
        extra += pieces(v)
    extra.append(jnp.zeros((10, feats), F32))
    z_ref[count:, :] = jnp.concatenate(extra, axis=0).astype(BF)
    for ref in (keep_ref, send_ref):
        ref[count:, half:] = jnp.zeros((16, units), F32)
    for one in copies:
        one.wait()
    p = jnp.dot(z_ref[...], w_ref[...], preferred_element_type=F32)
    low = c_ref[0] == 0
    keep_ref[:, :half] = jnp.where(low, p[:, :half], p[:, half:])
    send_ref[:, :half] = jnp.where(low, p[:, half:], p[:, :half])
    shift = jnp.sum(extra_ref[...].astype(F32), axis=0, keepdims=True)
    shift_ref[...] = jnp.where(low, shift[:, :half], shift[:, half:])


def first_layer(rows, gain, bias, w_all, c_ref, cols):
    n, feats = rows[0].shape
    count = 4 * n
    units = w_all[0].shape[1]
    shape = (count + 16, 3 * units)
    return pl.pallas_call(
        first_kernel,
        out_shape=[jax.ShapeDtypeStruct(shape, F32)] * 2
        + [jax.ShapeDtypeStruct((4 * units, cols), BF), jax.ShapeDtypeStruct((1, 2 * units), F32)],
        in_specs=[SMEM] + [VMEM] * 6 + [ANY] * 4,
        out_specs=[VMEM] * 4,
        scratch_shapes=[
            pltpu.VMEM((count + 16, feats), BF),
            pltpu.VMEM((feats, 4 * units), BF),
            pltpu.VMEM((16, 4 * units), BF),
            pltpu.SemaphoreType.DMA((8 + 4 * (cols // units),)),
        ],
        compiler_params=pltpu.CompilerParams(vmem_limit_bytes=32 << 20),
        cost_estimate=pl.CostEstimate(
            flops=2 * count * feats * 4 * units, bytes_accessed=4 << 20, transcendentals=0
        ),
        name="first_layer",
    )(c_ref, *rows, gain.reshape(1, -1), bias.reshape(1, -1), *w_all)


def pieces(v):
    out = []
    for _ in range(3):
        part = v.astype(BF).astype(F32)
        out.append(part)
        v = v - part
    return out


def pair_kernel(keep_ref, near_ref, out_ref):
    n = out_ref.shape[1] - 16
    count = 4 * n
    wide = out_ref.shape[2]
    half = wide * 2 // 3
    keep, near = keep_ref[:count, :half], near_ref[:count, :half]
    stats_a, stats_b = keep_ref[:count, half:], near_ref[:count, half:]
    mean_a, spread_a = stats_a[:, 0:1], stats_a[:, 1:2]
    mean_b, spread_b = stats_b[:, 0:1], stats_b[:, 1:2]
    tail_a, tail_b = keep_ref[count:, :half], near_ref[count:, :half]
    gain_a = jnp.sum(tail_a[0:3], axis=0, keepdims=True)
    gain_b = jnp.sum(tail_b[0:3], axis=0, keepdims=True)
    shift = jnp.sum(tail_a[3:6] + tail_b[3:6], axis=0, keepdims=True)
    apart = 0.5 * (mean_a - mean_b)
    mean = 0.5 * (mean_a + mean_b)
    spread = 0.5 * (spread_a + spread_b) + apart * apart
    summed = (keep + near + apart * (gain_a - gain_b)).astype(BF)
    columns = pieces(mean) + pieces(spread)
    lane = lax.broadcasted_iota(jnp.int32, (count, wide - half), 1)
    stats = jnp.zeros((count, wide - half), F32)
    for k, column in enumerate(columns):
        stats = jnp.where(lane == k, column, stats)
    stats = stats.astype(BF)
    lower = jnp.concatenate(
        pieces(gain_a + gain_b) + pieces(shift) + [jnp.zeros((10, half), F32)], axis=0
    )
    lower = jnp.concatenate([lower, jnp.zeros((16, wide - half), F32)], axis=1).astype(BF)
    for k in range(4):
        out_ref[k, :n, :half] = summed[k * n : (k + 1) * n]
        out_ref[k, :n, half:] = stats[k * n : (k + 1) * n]
        out_ref[k, n:, :] = lower


def pair_sum(keep, near):
    rows, wide = keep.shape
    n = (rows - 16) // 4
    return pl.pallas_call(
        pair_kernel,
        out_shape=jax.ShapeDtypeStruct((4, n + 16, wide), BF),
        in_specs=[VMEM, VMEM],
        out_specs=VMEM,
        compiler_params=pltpu.CompilerParams(vmem_limit_bytes=16 << 20),
        cost_estimate=pl.CostEstimate(
            flops=10 * rows * wide, bytes_accessed=1 << 20, transcendentals=0
        ),
        name="pair_sum",
    )(keep, near)


def second_kernel(c_ref, at_ref, own_ref, other_ref, w_ref, kept, s1, s2, s3, sum_ref):
    n = kept.shape[0]
    half = own_ref.shape[1]
    low = c_ref[0] == 0
    own, other = own_ref[...].astype(F32), other_ref[...].astype(F32)
    first = jnp.where(low, own, other).astype(BF)
    last = jnp.where(low, other, own).astype(BF)
    sum_ref[...] = jnp.dot(
        first, w_ref[:half, :], preferred_element_type=F32
    ) + jnp.dot(last, w_ref[half:, :], preferred_element_type=F32)
    for k, ref in enumerate((kept, s1, s2, s3)):
        ref[...] = sum_ref[pl.ds(pl.multiple_of(at_ref[k], n), n), :].astype(ref.dtype)


def second_layer(own, other, w_out, c_ref, at):
    count = own.shape[0]
    cols = w_out.shape[1]
    out = (count // 4, cols)
    return pl.pallas_call(
        second_kernel,
        out_shape=[jax.ShapeDtypeStruct(out, F32)] + [jax.ShapeDtypeStruct(out, BF)] * 3,
        in_specs=[SMEM, SMEM] + [VMEM] * 3,
        out_specs=[VMEM] * 4,
        scratch_shapes=[pltpu.VMEM((count, cols), F32)],
        compiler_params=pltpu.CompilerParams(vmem_limit_bytes=16 << 20),
        cost_estimate=pl.CostEstimate(
            flops=4 * count * own.shape[1] * cols, bytes_accessed=1 << 20, transcendentals=0
        ),
        name="second_layer",
    )(c_ref, at, own, other, w_out)


def local(
    patches,
    norm_gain,
    norm_bias,
    proj_in,
    proj_in_bias,
    proj_out,
    proj_out_bias,
    text_rows,
    out_grads,
    gate_weight,
    up_weight,
    down_weight,
    image_counts,
    image_sequence,
    image_offsets,
):
    g, zl, c, zh, x = (lax.axis_index(a) for a in ("g", "zl", "c", "zh", "x"))
    units = proj_in.shape[1]
    width = gate_weight.shape[1]
    cols = text_rows.shape[1]

    patch_other = swap(patches, "zh")
    packed = jnp.concatenate(
        [proj_in]
        + [proj_out[:, k * units : (k + 1) * units] for k in range(cols // units)]
        + [jnp.pad(three_parts(proj_in_bias), ((0, 13), (0, 0)))],
        axis=0,
    )
    w_all = line_of(packed, "g")
    pair = in_order(patches, patch_other, zh)
    rows = line_of(pair, "x")
    own = patches.shape[0]
    count = 8 * own

    side = jnp.concatenate([text_rows, out_grads], axis=1)
    side_other = swap(side, "zh")
    side_pair = in_order(side, side_other, zh)
    side_all = copy_for_each(side_pair, "x").reshape(count, 2 * cols)
    text, cotangent = side_all[:, :cols], side_all[:, cols:]

    half = 2 * units
    c_ref = c.reshape(1).astype(jnp.int32)
    keep, send, w_out, bias = first_layer(rows, norm_gain, norm_bias, w_all, c_ref, cols)
    near = swap(send, "c")
    turns = jnp.arange(4, dtype=jnp.int32)
    n = 2 * own
    parts = lax.all_to_all(pair_sum(keep, near), "zl", 0, 0, tiled=True).astype(F32)
    means = jnp.sum(parts[:, :n, half : half + 3], axis=2, keepdims=True)
    spreads = jnp.sum(parts[:, :n, half + 3 : half + 6], axis=2, keepdims=True)
    gains = jnp.sum(parts[:, n : n + 3, :half], axis=1, keepdims=True)
    shift = jnp.sum(parts[:, n + 3 : n + 6, :half], axis=(0, 1))
    mean = jnp.mean(means, axis=0, keepdims=True)
    spread = jnp.mean(spreads + (means - mean) * (means - mean), axis=0)
    total = jnp.sum(parts[:, :n, :half] + (means - mean) * gains, axis=0)
    total = total * lax.rsqrt(spread + 1e-05) + (shift + bias[0])
    activated = jax.nn.gelu(total, approximate=False).astype(BF)
    act_own = jnp.concatenate(line_of(activated, "zl"), axis=0)
    act_other = swap(act_own, "c")

    part, *sent = second_layer(act_own, act_other, w_out, c_ref, (-turns - zl) % 4 * n)
    for k, v in enumerate(sent):
        part = part + from_next(v, "x", k + 1).astype(F32)
    part = part + swap(part.astype(BF), "zh").astype(F32)
    pair_projected = (part + proj_out_bias).astype(BF)
    projected = jnp.where(zh == 0, pair_projected[:own], pair_projected[own:])
    line_rows = jnp.concatenate(line_of(pair_projected, "x"), axis=0)
    far_rows = [from_next(line_rows, "g", k) for k in (1, 2, 3)]

    q = jnp.arange(count, dtype=jnp.int32)
    block = ((zl + (q // own) % 4) % 4) * 2 + (c + q // (4 * own)) % 2
    at = block * own + q % own
    source, covered = seq_sources(image_counts, image_sequence, image_offsets, g * count + at)

    def gathered_place(r):
        return (r // own) % 4 * (2 * own) + (r // (4 * own)) % 2 * own + r % own

    place = gathered_place(at)

    def x_turned(p):
        return (p - x * (2 * own)) % count

    column = jnp.where(
        covered,
        (source // count - g) % 4 * count + x_turned(gathered_place(source % count)),
        4 * count + place,
    )
    column = lax.optimization_barrier(column)
    choose = column[:, None]
    near_choice = jnp.concatenate([choose == q[None, :], choose == q[None, :] + 4 * count], axis=1)
    far_choice = choose == count + jnp.arange(3 * count)[None, :]
    near_inputs = mm(near_choice.astype(BF), jnp.concatenate([line_rows, text], axis=0))
    far_inputs = mm(far_choice.astype(BF), jnp.concatenate(far_rows, axis=0))
    inputs = (near_inputs + far_inputs).astype(BF)
    z_block = q // own % 4 * 2 + (c + q // (4 * own)) % 2
    reorder = (gathered_place(z_block * own + q % own)[:, None] == q[None, :]).astype(BF)
    back_rows = pick(reorder, cotangent)

    given = mm_t(back_rows[4 * own :], down_weight)
    hidden = mm_t(back_rows[: 4 * own], down_weight)
    there = swap(given, "c")
    near = (hidden + there).astype(BF).reshape(4, own, width)
    hidden_grad = jnp.sum(lax.all_to_all(near, "zl", 0, 0, tiled=True).astype(F32), axis=0)
    whole = jnp.concatenate([mm(inputs, gate_weight), mm(inputs, up_weight)], axis=1)
    total = row_share(whole[: 4 * own], whole[4 * own :], own)
    gate_grad, up_grad = unit_grads(total[:, :width], total[:, width:], hidden_grad)

    grads = jnp.concatenate([gate_grad, up_grad], axis=1)
    line = jnp.concatenate([grads] + [from_next(grads, "zl", k) for k in (1, 2, 3)], axis=0)
    other = swap(line, "c")
    halves = [
        mm_t(h[:, :width], gate_weight) + mm_t(h[:, width:], up_weight) for h in (line, other)
    ]
    turned = jnp.concatenate(halves, axis=0).astype(BF)

    def image_rows(k):
        base = (g - k) % 4 * count
        row = base + (x - q // (2 * own)) % 4 * own + q // own % 2 * (4 * own) + q % own
        target, valid = image_targets(image_counts, image_sequence, image_offsets, row)
        held = valid & (target // count == g)
        return (held[:, None] & ((target % count)[:, None] == at[None, :])).astype(BF)

    back = []
    for k in (2, 1, 3):
        given = pick(image_rows(k), turned)
        back.append(from_next(given, "g", k))
    restore = (q[:, None] == ((x - place // n) % 4 * n + place % n)[None, :]).astype(BF)
    ordered = pick(restore, turned)
    image = mm(image_rows(0), turned) + sum(b.astype(F32) for b in back)
    image = image.astype(BF)
    both = [
        jnp.concatenate([v[k * n : (k + 1) * n] for v in (ordered, image)], axis=0)
        for k in range(4)
    ]
    part = both[0].astype(F32)
    for k in (2, 1, 3):
        part = part + from_next(both[k], "x", k).astype(F32)
    part = part.reshape(2, 2, own, cols)
    keep = jnp.where(zh == 0, part[:, 0], part[:, 1])
    give = jnp.where(zh == 0, part[:, 1], part[:, 0]).astype(BF)
    final = (keep + swap(give, "zh").astype(F32)).astype(BF)
    sequence_grads, row_grads = final[0], final[1]
    return (projected, sequence_grads, row_grads)


def solution(mesh):
    finer = Mesh(mesh.devices.reshape(4, 4, 2, 2, 4), ("g", "zl", "c", "zh", "x"))
    in_specs = (
        P(ROWS, DP),
        P(DP),
        P(DP),
        P(DP, ROWS),
        P(ROWS),
        P(ROWS, DP),
        P(DP),
        P(ROWS, DP),
        P(ROWS, DP),
        P(DP, MP),
        P(DP, MP),
        P(MP, DP),
        P(),
        P(),
        P(),
    )
    out_specs = (P(ROWS, DP), P(ROWS, DP), P(ROWS, DP))
    return jax.shard_map(local, mesh=finer, in_specs=in_specs, out_specs=out_specs, check_vma=False)
```

profile of v0, /device:TPU:32, one launch (start us, length us, event | category | flops | bytes accessed | tf_op | source)
XLA Modules:
  0.0 225.2 jit_solution(17626349603594637707)
XLA Ops:
  0.6 6.4 %collective-permute-start = (bf16[32,1600]{1,0:T(8,128)(2,1)}, bf16[32,1600]{1,0:T(8,128)(2,1)S(1)}, u32[]{:S(2)}, u32[]{:S(2)}) collective-permute-start(bf16[32,1600]{1,0:T(8,128)(2,1)} %param.15), channel_id=1, source_target_pairs={{0,4},{4,0},{1,5},{5,1},{2,6},{6,2},{3,7},{7,3},{8,12},{12,8},{9,1... | collective-permute-start | bytes 307208 | tf_op jit(solution)/shard_map/ppermute | solution.py:24
  7.7 1.0 constant_dynamic-update-slice_fusion.1
  11.8 1.6 collective-permute-start.6
  13.5 2.9 %collective-permute-start.5 = (bf16[2128,128]{1,0:T(8,128)(2,1)S(1)}, bf16[2128,128]{1,0:T(8,128)(2,1)}, u32[]{:S(2)}, u32[]{:S(2)}) collective-permute-start(bf16[2128,128]{1,0:T(8,128)(2,1)S(1)} %constant_dynamic-update-slice_fusion.w0), channel_id=1, source_target_pairs={{128,0},{192,64},{0,128},{64,192},{129,1},{193,65},{1,129},{65,193... | collective-permute-start | bytes 1634312 | tf_op jit(solution)/shard_map/ppermute | solution.py:20
  16.4 1.3 collective-permute-start.4
  18.7 1.6 collective-permute-start.3
  22.6 1.4 constant_dynamic-update-slice_fusion.3
  24.0 2.7 %collective-permute-start.2 = (bf16[64,1600]{1,0:T(8,128)(2,1)S(1)}, bf16[64,1600]{1,0:T(8,128)(2,1)S(1)}, u32[]{:S(2)}, u32[]{:S(2)}) collective-permute-start(bf16[64,1600]{1,0:T(8,128)(2,1)S(1)} %maximum_select_fusion.x0), channel_id=1, source_target_pairs={{2,0},{3,1},{0,2},{1,3},{6,4},{7,5},{4,6},{5,7},{10,8},{11,9},{8,1... | collective-permute-start | bytes 614408 | tf_op jit(solution)/shard_map/ppermute | solution.py:20
  26.7 1.4 collective-permute-start.1
  28.2 1.4 constant_dynamic-update-slice_fusion.2
  29.6 1.9 collective-permute-done.2.x2
  31.9 2.9 %collective-permute-done.1.x1 = bf16[64,1600]{1,0:T(8,128)(2,1)S(1)} collective-permute-done((bf16[64,1600]{1,0:T(8,128)(2,1)S(1)}, bf16[64,1600]{1,0:T(8,128)(2,1)S(1)}, u32[]{:S(2)}, u32[]{:S(2)}) %collective-permute-start.1) | collective-permute-done | bytes 204832 | tf_op jit(solution)/shard_map/ppermute | solution.py:20
  34.7 5.2 %collective-permute-done.5.w2 = bf16[2128,128]{1,0:T(8,128)(2,1)} collective-permute-done((bf16[2128,128]{1,0:T(8,128)(2,1)S(1)}, bf16[2128,128]{1,0:T(8,128)(2,1)}, u32[]{:S(2)}, u32[]{:S(2)}) %collective-permute-start.5) | collective-permute-done | bytes 544800 | tf_op jit(solution)/shard_map/ppermute | solution.py:20
  39.9 4.2 %first_layer.1 = (f32[272,384]{1,0:T(8,128)S(1)}, f32[272,384]{1,0:T(8,128)S(1)}, bf16[512,512]{1,0:T(8,128)(2,1)S(1)}, f32[1,256]{1,0:T(1,128)S(1)}) custom-call(s32[1]{0:T(128)} %bitcast.c_ref, bf16[64,1600]{1,0:T(8,128)(2,1)S(1)} %maximum_select_fusion.x0, bf16[64,1600]{1,0:T(8,128)(2,1)S(1)} %collective-permute-done.1.x1, ...), custom_call_target="tpu_custom_call" | custom-call | flops 419430400 | bytes 4194304 | tf_op jit(solution)/shard_map/first_layer/pallas_call | solution.py:178
  45.1 1.7 collective-permute-done.7.near_ref
  47.7 4.5 %all-to-all-start = ((bf16[4,80,384]{2,1,0:T(8,128)(2,1)}), bf16[4,80,384]{2,1,0:T(8,128)(2,1)S(1)}, u32[]{:S(2)}, u32[]{:S(2)}) async-start(bf16[4,80,384]{2,1,0:T(8,128)(2,1)} %pair_sum.1), calls=%async_computation | async-start | bytes 491520 | tf_op jit(solution)/shard_map/all_to_all | solution.py:335
  53.1 6.4 %all-to-all-done = bf16[4,80,384]{2,1,0:T(8,128)(2,1)S(1)} async-done(((bf16[4,80,384]{2,1,0:T(8,128)(2,1)}), bf16[4,80,384]{2,1,0:T(8,128)(2,1)S(1)}, u32[]{:S(2)}, u32[]{:S(2)}) %all-to-all-start) | async-done | bytes 245792 | tf_op jit(solution)/shard_map/all_to_all | solution.py:335
  60.6 3.9 %collective-permute-start.9 = (bf16[64,256]{1,0:T(8,128)(2,1)S(1)}, bf16[64,256]{1,0:T(8,128)(2,1)S(1)}, u32[]{:S(2)}, u32[]{:S(2)}) collective-permute-start(bf16[64,256]{1,0:T(8,128)(2,1)S(1)} %fusion.62), channel_id=1, source_target_pairs={{32,0},{48,16},{0,32},{16,48},{33,1},{49,17},{1,33},{17,49},{34,2}... | collective-permute-start | bytes 98312 | tf_op jit(solution)/shard_map/ppermute | solution.py:20
  64.5 2.2 collective-permute-done.9
  66.8 1.7 collective-permute-done.8
  68.7 1.2 collective-permute-done.11.other_ref
  70.8 2.8 %collective-permute-start.12 = (bf16[64,512]{1,0:T(8,128)(2,1)S(1)}, bf16[64,512]{1,0:T(8,128)(2,1)S(1)}, u32[]{:S(2)}, u32[]{:S(2)}) collective-permute-start(bf16[64,512]{1,0:T(8,128)(2,1)S(1)} %get-tuple-element.16), channel_id=1, source_target_pairs={{1,0},{2,1},{3,2},{0,3},{5,4},{6,5},{7,6},{4,7},{9,8},{10,9},{11,1... | collective-permute-start | bytes 196616 | tf_op jit(solution)/shard_map/ppermute | solution.py:20
  76.8 2.9 %collective-permute-done.13 = bf16[64,512]{1,0:T(8,128)(2,1)S(1)} collective-permute-done((bf16[64,512]{1,0:T(8,128)(2,1)S(1)}, bf16[64,512]{1,0:T(8,128)(2,1)S(1)}, u32[]{:S(2)}, u32[]{:S(2)}) %collective-permute-start.13) | collective-permute-done | bytes 65568 | tf_op jit(solution)/shard_map/ppermute | solution.py:20
  80.4 1.1 collective-permute-start.15
  82.2 7.0 %collective-permute-done.15 = bf16[64,512]{1,0:T(8,128)(2,1)S(1)} collective-permute-done((bf16[64,512]{1,0:T(8,128)(2,1)S(1)}, bf16[64,512]{1,0:T(8,128)(2,1)S(1)}, u32[]{:S(2)}, u32[]{:S(2)}) %collective-permute-start.15) | collective-permute-done | bytes 65568 | tf_op jit(solution)/shard_map/ppermute | solution.py:24
  89.3 1.6 collective-permute-start.19
  90.8 2.1 collective-permute-start.18
  94.7 3.8 %all-to-all-start.1 = ((bf16[4,64,1024]{2,1,0:T(8,128)(2,1)}), bf16[4,64,1024]{2,1,0:T(8,128)(2,1)S(1)}, u32[]{:S(2)}, u32[]{:S(2)}) async-start(bf16[4,64,1024]{2,1,0:T(8,128)(2,1)} %broadcast_in_dim.9), calls=%async_computation.1 | async-start | bytes 1048576 | tf_op jit(solution)/shard_map/all_to_all | solution.py:29
  98.6 1.3 collective-permute-start.23
  99.9 2.4 %collective-permute-start.22 = (bf16[256,512]{1,0:T(8,128)(2,1)S(1)}, bf16[256,512]{1,0:T(8,128)(2,1)}, u32[]{:S(2)}, u32[]{:S(2)}) collective-permute-start(bf16[256,512]{1,0:T(8,128)(2,1)S(1)} %pad_maximum_fusion.2), channel_id=1, source_target_pairs={{128,0},{192,64},{0,128},{64,192},{129,1},{193,65},{1,129},{65,193... | collective-permute-start | bytes 786440 | tf_op jit(solution)/shard_map/ppermute | solution.py:20
  102.3 1.6 collective-permute-start.21
  103.9 2.7 %all-to-all-done.1 = bf16[4,64,1024]{2,1,0:T(8,128)(2,1)S(1)} async-done(((bf16[4,64,1024]{2,1,0:T(8,128)(2,1)}), bf16[4,64,1024]{2,1,0:T(8,128)(2,1)S(1)}, u32[]{:S(2)}, u32[]{:S(2)}) %all-to-all-start.1) | async-done | bytes 524320 | tf_op jit(solution)/shard_map/all_to_all | solution.py:29
  106.6 1.5 collective-permute-done.23
  108.1 2.8 %collective-permute-done.22 = bf16[256,512]{1,0:T(8,128)(2,1)} collective-permute-done((bf16[256,512]{1,0:T(8,128)(2,1)S(1)}, bf16[256,512]{1,0:T(8,128)(2,1)}, u32[]{:S(2)}, u32[]{:S(2)}) %collective-permute-start.22) | collective-permute-done | bytes 262176 | tf_op jit(solution)/shard_map/ppermute | solution.py:20
  111.2 1.5 fusion.6
  115.8 1.4 pad_maximum_fusion
  119.7 3.4 %collective-permute-done.17 = f32[128,1792]{1,0:T(8,128)S(1)} collective-permute-done((f32[128,1792]{1,0:T(8,128)S(1)}, f32[128,1792]{1,0:T(8,128)S(1)}, u32[]{:S(2)}, u32[]{:S(2)}) %collective-permute-start.17) | collective-permute-done | bytes 917536 | tf_op jit(solution)/shard_map/ppermute | solution.py:24
  123.1 1.5 fusion
  124.6 4.6 %all-to-all-start.2 = ((bf16[4,32,1792]{2,1,0:T(8,128)(2,1)}), bf16[4,32,1792]{2,1,0:T(8,128)(2,1)S(1)}, u32[]{:S(2)}, u32[]{:S(2)}) async-start(bf16[4,32,1792]{2,1,0:T(8,128)(2,1)} %bitcast.7), calls=%async_computation.2 | async-start | bytes 917504 | tf_op jit(solution)/shard_map/all_to_all | solution.py:390
  129.2 3.5 %fusion.128 = (bf16[128,3584]{1,0:T(8,128)(2,1)S(1)}, f32[128,3584]{1,0:T(8,128)}) fusion(f32[128,3584]{1,0:T(8,128)} %collective-permute-done.24, f32[256,1792]{1,0:T(8,128)} %copy-done.5, f32[256,1792]{1,0:T(8,128)} %copy-done.6), kind=kLoop, calls=%fused_computation.353 | loop fusion | flops 1376256 | bytes 8257536 | tf_op jit(solution)/shard_map/convert.2
  133.4 2.0 collective-permute-start.27
  135.5 4.2 %collective-permute-start.26 = (bf16[32,3584]{1,0:T(8,128)(2,1)S(1)}, bf16[32,3584]{1,0:T(8,128)(2,1)S(1)}, u32[]{:S(2)}, u32[]{:S(2)}) collective-permute-start(bf16[32,3584]{1,0:T(8,128)(2,1)S(1)} %get-tuple-element.41), channel_id=1, source_target_pairs={{32,0},{48,16},{0,32},{16,48},{33,1},{49,17},{1,33},{17,49},{34,2}... | collective-permute-start | bytes 688136 | tf_op jit(solution)/shard_map/ppermute | solution.py:20
  139.7 5.7 %all-to-all-done.2 = bf16[4,32,1792]{2,1,0:T(8,128)(2,1)S(1)} async-done(((bf16[4,32,1792]{2,1,0:T(8,128)(2,1)}), bf16[4,32,1792]{2,1,0:T(8,128)(2,1)S(1)}, u32[]{:S(2)}, u32[]{:S(2)}) %all-to-all-start.2) | async-done | bytes 458784 | tf_op jit(solution)/shard_map/all_to_all | solution.py:390
  145.4 11.4 %collective-permute-done.25 = bf16[32,3584]{1,0:T(8,128)(2,1)S(1)} collective-permute-done((bf16[32,3584]{1,0:T(8,128)(2,1)}, bf16[32,3584]{1,0:T(8,128)(2,1)S(1)}, u32[]{:S(2)}, u32[]{:S(2)}) %collective-permute-start.25) | collective-permute-done | bytes 229408 | tf_op jit(solution)/shard_map/ppermute | solution.py:20
  156.8 2.0 collective-permute-done.26
  158.9 1.1 fusion.23
  160.2 1.5 collective-permute-start.30
  161.7 4.3 %collective-permute-start.29 = (bf16[32,3584]{1,0:T(8,128)(2,1)S(1)}, bf16[32,3584]{1,0:T(8,128)(2,1)S(1)}, u32[]{:S(2)}, u32[]{:S(2)}) collective-permute-start(bf16[32,3584]{1,0:T(8,128)(2,1)S(1)} %pad_maximum_fusion.4), channel_id=1, source_target_pairs={{32,0},{48,16},{0,32},{16,48},{33,1},{49,17},{1,33},{17,49},{34,2}... | collective-permute-start | bytes 688136 | tf_op jit(solution)/shard_map/ppermute | solution.py:20
  166.0 4.0 %collective-permute-done.30 = bf16[32,3584]{1,0:T(8,128)(2,1)S(1)} collective-permute-done((bf16[32,3584]{1,0:T(8,128)(2,1)S(1)}, bf16[32,3584]{1,0:T(8,128)(2,1)S(1)}, u32[]{:S(2)}, u32[]{:S(2)}) %collective-permute-start.30) | collective-permute-done | bytes 229408 | tf_op jit(solution)/shard_map/ppermute | solution.py:20
  170.0 10.5 %collective-permute-done.29 = bf16[32,3584]{1,0:T(8,128)(2,1)S(1)} collective-permute-done((bf16[32,3584]{1,0:T(8,128)(2,1)S(1)}, bf16[32,3584]{1,0:T(8,128)(2,1)S(1)}, u32[]{:S(2)}, u32[]{:S(2)}) %collective-permute-start.29) | collective-permute-done | bytes 229408 | tf_op jit(solution)/shard_map/ppermute | solution.py:20
  180.5 4.0 %collective-permute-done.28 = bf16[32,3584]{1,0:T(8,128)(2,1)S(1)} collective-permute-done((bf16[32,3584]{1,0:T(8,128)(2,1)S(1)}, bf16[32,3584]{1,0:T(8,128)(2,1)S(1)}, u32[]{:S(2)}, u32[]{:S(2)}) %collective-permute-start.28) | collective-permute-done | bytes 229408 | tf_op jit(solution)/shard_map/ppermute | solution.py:20
  188.9 1.8 collective-permute-start.34
  190.9 1.6 collective-permute-start.33
  192.8 1.5 collective-permute-start.32
  194.6 3.9 %collective-permute-done.34 = bf16[256,512]{1,0:T(8,128)(2,1)S(1)} collective-permute-done((bf16[256,512]{1,0:T(8,128)(2,1)S(1)}, bf16[256,512]{1,0:T(8,128)(2,1)S(1)}, u32[]{:S(2)}, u32[]{:S(2)}) %collective-permute-start.34) | collective-permute-done | bytes 262176 | tf_op jit(solution)/shard_map/ppermute | solution.py:20
  198.5 1.7 collective-permute-done.33
  200.2 4.8 %collective-permute-done.32 = bf16[256,512]{1,0:T(8,128)(2,1)S(1)} collective-permute-done((bf16[256,512]{1,0:T(8,128)(2,1)S(1)}, bf16[256,512]{1,0:T(8,128)(2,1)S(1)}, u32[]{:S(2)}, u32[]{:S(2)}) %collective-permute-start.32) | collective-permute-done | bytes 262176 | tf_op jit(solution)/shard_map/ppermute | solution.py:20
  205.3 3.3 %collective-permute-start.35 = (bf16[128,512]{1,0:T(8,128)(2,1)S(1)}, bf16[128,512]{1,0:T(8,128)(2,1)S(1)}, u32[]{:S(2)}, u32[]{:S(2)}) collective-permute-start(bf16[128,512]{1,0:T(8,128)(2,1)S(1)} %pad_maximum_fusion.6), channel_id=1, source_target_pairs={{2,0},{3,1},{0,2},{1,3},{6,4},{7,5},{4,6},{5,7},{10,8},{11,9},{8,1... | collective-permute-start | bytes 393224 | tf_op jit(solution)/shard_map/ppermute | solution.py:20
  208.7 1.3 collective-permute-start.36
  210.9 1.8 collective-permute-done.35
  212.7 2.0 collective-permute-done.36
  214.7 1.5 collective-permute-done.37
  216.3 1.1 collective-permute-start.38
  218.0 6.5 %collective-permute-done.38 = bf16[2,32,512]{2,1,0:T(8,128)(2,1)S(1)} collective-permute-done((bf16[2,32,512]{2,1,0:T(8,128)(2,1)S(1)}, bf16[2,32,512]{2,1,0:T(8,128)(2,1)S(1)}, u32[]{:S(2)}, u32[]{:S(2)}) %collective-permute-start.38) | collective-permute-done | bytes 65568 | tf_op jit(solution)/shard_map/ppermute | solution.py:24
  (158 shorter events, 33.4 us)
Async XLA Ops:
  0.6 112.4 %copy-start = (bf16[512,1792]{1,0:T(8,128)(2,1)S(1)}, bf16[512,1792]{1,0:T(8,128)(2,1)}, u32[]{:S(2)}) copy-start(bf16[512,1792]{1,0:T(8,128)(2,1)} %param.25) | copy-start | bytes 5505028
  0.6 17.1 %collective-permute-start = (bf16[32,1600]{1,0:T(8,128)(2,1)}, bf16[32,1600]{1,0:T(8,128)(2,1)S(1)}, u32[]{:S(2)}, u32[]{:S(2)}) collective-permute-start(bf16[32,1600]{1,0:T(8,128)(2,1)} %param.15), channel_id=1, source_target_pairs={{0,4},{4,0},{1,5},{5,1},{2,6},{6,2},{3,7},{7,3},{8,12},{12,8},{9,1... | collective-permute-start | bytes 307208 | tf_op jit(solution)/shard_map/ppermute | solution.py:24
  11.8 22.9 %collective-permute-start.6 = (bf16[2128,128]{1,0:T(8,128)(2,1)S(1)}, bf16[2128,128]{1,0:T(8,128)(2,1)S(1)}, u32[]{:S(2)}, u32[]{:S(2)}) collective-permute-start(bf16[2128,128]{1,0:T(8,128)(2,1)S(1)} %constant_dynamic-update-slice_fusion.w0), channel_id=1, source_target_pairs={{192,0},{0,64},{64,128},{128,192},{193,1},{1,65},{65,129},{129,193... | collective-permute-start | bytes 1634312 | tf_op jit(solution)/shard_map/ppermute | solution.py:20
  13.5 26.5 %collective-permute-start.5 = (bf16[2128,128]{1,0:T(8,128)(2,1)S(1)}, bf16[2128,128]{1,0:T(8,128)(2,1)}, u32[]{:S(2)}, u32[]{:S(2)}) collective-permute-start(bf16[2128,128]{1,0:T(8,128)(2,1)S(1)} %constant_dynamic-update-slice_fusion.w0), channel_id=1, source_target_pairs={{128,0},{192,64},{0,128},{64,192},{129,1},{193,65},{1,129},{65,193... | collective-permute-start | bytes 1634312 | tf_op jit(solution)/shard_map/ppermute | solution.py:20
  16.4 23.6 %collective-permute-start.4 = (bf16[2128,128]{1,0:T(8,128)(2,1)S(1)}, bf16[2128,128]{1,0:T(8,128)(2,1)}, u32[]{:S(2)}, u32[]{:S(2)}) collective-permute-start(bf16[2128,128]{1,0:T(8,128)(2,1)S(1)} %constant_dynamic-update-slice_fusion.w0), channel_id=1, source_target_pairs={{64,0},{128,64},{192,128},{0,192},{65,1},{129,65},{193,129},{1,193... | collective-permute-start | bytes 1634312 | tf_op jit(solution)/shard_map/ppermute | solution.py:20
  17.7 27.3 %copy-start.16 = (s32[16]{0:T(128)S(1)}, s32[16]{0:T(128)}, u32[]{:S(2)}) copy-start(s32[16]{0:T(128)} %param.29) | copy-start | bytes 196
  17.7 27.4 %copy-start.17 = (s32[16]{0:T(128)S(1)}, s32[16]{0:T(128)}, u32[]{:S(2)}) copy-start(s32[16]{0:T(128)} %param.28) | copy-start | bytes 196
  17.7 27.4 %copy-start.20 = (s32[16]{0:T(128)S(1)}, s32[16]{0:T(128)}, u32[]{:S(2)}) copy-start(s32[16]{0:T(128)} %param.27) | copy-start | bytes 196
  18.7 8.0 %collective-permute-start.3 = (bf16[64,1600]{1,0:T(8,128)(2,1)S(1)}, bf16[64,1600]{1,0:T(8,128)(2,1)S(1)}, u32[]{:S(2)}, u32[]{:S(2)}) collective-permute-start(bf16[64,1600]{1,0:T(8,128)(2,1)S(1)} %maximum_select_fusion.x0), channel_id=1, source_target_pairs={{3,0},{0,1},{1,2},{2,3},{7,4},{4,5},{5,6},{6,7},{11,8},{8,9},{9,10... | collective-permute-start | bytes 614408 | tf_op jit(solution)/shard_map/ppermute | solution.py:20
  22.6 29.6 %copy-start.12 = (s32[16]{0:T(128)}, s32[16]{0:T(128)S(1)}, u32[]{:S(2)}) copy-start(s32[16]{0:T(128)S(1)} %reduce.4) | copy-start | bytes 196
  24.0 7.5 %collective-permute-start.2 = (bf16[64,1600]{1,0:T(8,128)(2,1)S(1)}, bf16[64,1600]{1,0:T(8,128)(2,1)S(1)}, u32[]{:S(2)}, u32[]{:S(2)}) collective-permute-start(bf16[64,1600]{1,0:T(8,128)(2,1)S(1)} %maximum_select_fusion.x0), channel_id=1, source_target_pairs={{2,0},{3,1},{0,2},{1,3},{6,4},{7,5},{4,6},{5,7},{10,8},{11,9},{8,1... | collective-permute-start | bytes 614408 | tf_op jit(solution)/shard_map/ppermute | solution.py:20
  26.7 8.0 %collective-permute-start.1 = (bf16[64,1600]{1,0:T(8,128)(2,1)S(1)}, bf16[64,1600]{1,0:T(8,128)(2,1)S(1)}, u32[]{:S(2)}, u32[]{:S(2)}) collective-permute-start(bf16[64,1600]{1,0:T(8,128)(2,1)S(1)} %maximum_select_fusion.x0), channel_id=1, source_target_pairs={{1,0},{2,1},{3,2},{0,3},{5,4},{6,5},{7,6},{4,7},{9,8},{10,9},{11,1... | collective-permute-start | bytes 614408 | tf_op jit(solution)/shard_map/ppermute | solution.py:20
  31.5 61.4 %collective-permute-start.16 = (bf16[32,1024]{1,0:T(8,128)(2,1)}, bf16[32,1024]{1,0:T(8,128)(2,1)}, u32[]{:S(2)}, u32[]{:S(2)}) collective-permute-start(bf16[32,1024]{1,0:T(8,128)(2,1)} %constant_dynamic-update-slice_fusion.2), channel_id=1, source_target_pairs={{0,4},{4,0},{1,5},{5,1},{2,6},{6,2},{3,7},{7,3},{8,12},{12,8},{9,1... | collective-permute-start | bytes 196616 | tf_op jit(solution)/shard_map/ppermute | solution.py:24
  44.2 0.8 copy-start.1
  45.0 24.9 %copy-start.2 = (bf16[512,512]{1,0:T(8,128)(2,1)S(1)}, bf16[512,512]{1,0:T(8,128)(2,1)}, u32[]{:S(2)}) copy-start(bf16[512,512]{1,0:T(8,128)(2,1)} %copy-done.1) | copy-start | bytes 1572868
  45.0 1.8 collective-permute-start.7
  45.1 25.7 %copy-start.14 = (s32[16]{0:T(128)}, s32[16]{0:T(128)S(1)}, u32[]{:S(2)}) copy-start(s32[16]{0:T(128)S(1)} %get-tuple-element.57) | copy-start | bytes 196
  47.7 41.4 %copy-start.19 = (f32[512]{0:T(512)S(1)}, f32[512]{0:T(512)}, u32[]{:S(2)}) copy-start(f32[512]{0:T(512)} %param.21) | copy-start | bytes 6148
  47.7 11.7 %all-to-all-start = ((bf16[4,80,384]{2,1,0:T(8,128)(2,1)}), bf16[4,80,384]{2,1,0:T(8,128)(2,1)S(1)}, u32[]{:S(2)}, u32[]{:S(2)}) async-start(bf16[4,80,384]{2,1,0:T(8,128)(2,1)} %pair_sum.1), calls=%async_computation | async-start | bytes 491520 | tf_op jit(solution)/shard_map/all_to_all | solution.py:335
  53.1 29.1 %copy-start.18 = (s32[256]{0:T(256)}, s32[256]{0:T(256)S(1)}, u32[]{:S(2)}) copy-start(s32[256]{0:T(256)S(1)} %fusion.84) | copy-start | bytes 3076
  60.2 4.3 %collective-permute-start.10 = (bf16[64,256]{1,0:T(8,128)(2,1)S(1)}, bf16[64,256]{1,0:T(8,128)(2,1)S(1)}, u32[]{:S(2)}, u32[]{:S(2)}) collective-permute-start(bf16[64,256]{1,0:T(8,128)(2,1)S(1)} %fusion.62), channel_id=1, source_target_pairs={{48,0},{0,16},{16,32},{32,48},{49,1},{1,17},{17,33},{33,49},{50,2}... | collective-permute-start | bytes 98312 | tf_op jit(solution)/shard_map/ppermute | solution.py:20
  60.6 6.2 %collective-permute-start.9 = (bf16[64,256]{1,0:T(8,128)(2,1)S(1)}, bf16[64,256]{1,0:T(8,128)(2,1)S(1)}, u32[]{:S(2)}, u32[]{:S(2)}) collective-permute-start(bf16[64,256]{1,0:T(8,128)(2,1)S(1)} %fusion.62), channel_id=1, source_target_pairs={{32,0},{48,16},{0,32},{16,48},{33,1},{49,17},{1,33},{17,49},{34,2}... | collective-permute-start | bytes 98312 | tf_op jit(solution)/shard_map/ppermute | solution.py:20
  64.5 3.9 %collective-permute-start.8 = (bf16[64,256]{1,0:T(8,128)(2,1)S(1)}, bf16[64,256]{1,0:T(8,128)(2,1)S(1)}, u32[]{:S(2)}, u32[]{:S(2)}) collective-permute-start(bf16[64,256]{1,0:T(8,128)(2,1)S(1)} %fusion.62), channel_id=1, source_target_pairs={{16,0},{32,16},{48,32},{0,48},{17,1},{33,17},{49,33},{1,49},{18,2}... | collective-permute-start | bytes 98312 | tf_op jit(solution)/shard_map/ppermute | solution.py:20
  68.4 1.4 collective-permute-start.11
  70.8 6.1 %collective-permute-start.12 = (bf16[64,512]{1,0:T(8,128)(2,1)S(1)}, bf16[64,512]{1,0:T(8,128)(2,1)S(1)}, u32[]{:S(2)}, u32[]{:S(2)}) collective-permute-start(bf16[64,512]{1,0:T(8,128)(2,1)S(1)} %get-tuple-element.16), channel_id=1, source_target_pairs={{1,0},{2,1},{3,2},{0,3},{5,4},{6,5},{7,6},{4,7},{9,8},{10,9},{11,1... | collective-permute-start | bytes 196616 | tf_op jit(solution)/shard_map/ppermute | solution.py:20
  73.6 6.1 %collective-permute-start.13 = (bf16[64,512]{1,0:T(8,128)(2,1)S(1)}, bf16[64,512]{1,0:T(8,128)(2,1)S(1)}, u32[]{:S(2)}, u32[]{:S(2)}) collective-permute-start(bf16[64,512]{1,0:T(8,128)(2,1)S(1)} %get-tuple-element.17), channel_id=1, source_target_pairs={{2,0},{3,1},{0,2},{1,3},{6,4},{7,5},{4,6},{5,7},{10,8},{11,9},{8,1... | collective-permute-start | bytes 196616 | tf_op jit(solution)/shard_map/ppermute | solution.py:20
  74.4 6.0 %collective-permute-start.14 = (bf16[64,512]{1,0:T(8,128)(2,1)S(1)}, bf16[64,512]{1,0:T(8,128)(2,1)S(1)}, u32[]{:S(2)}, u32[]{:S(2)}) collective-permute-start(bf16[64,512]{1,0:T(8,128)(2,1)S(1)} %get-tuple-element.18), channel_id=1, source_target_pairs={{3,0},{0,1},{1,2},{2,3},{7,4},{4,5},{5,6},{6,7},{11,8},{8,9},{9,10... | collective-permute-start | bytes 196616 | tf_op jit(solution)/shard_map/ppermute | solution.py:20
  80.4 8.7 %collective-permute-start.15 = (bf16[64,512]{1,0:T(8,128)(2,1)S(1)}, bf16[64,512]{1,0:T(8,128)(2,1)S(1)}, u32[]{:S(2)}, u32[]{:S(2)}) collective-permute-start(bf16[64,512]{1,0:T(8,128)(2,1)S(1)} %fusion.75), channel_id=1, source_target_pairs={{0,4},{4,0},{1,5},{5,1},{2,6},{6,2},{3,7},{7,3},{8,12},{12,8},{9,1... | collective-permute-start | bytes 196616 | tf_op jit(solution)/shard_map/ppermute | solution.py:24
  89.2 9.4 %collective-permute-start.20 = (bf16[64,512]{1,0:T(8,128)(2,1)S(1)}, bf16[64,512]{1,0:T(8,128)(2,1)S(1)}, u32[]{:S(2)}, u32[]{:S(2)}) collective-permute-start(bf16[64,512]{1,0:T(8,128)(2,1)S(1)} %get-tuple-element.36), channel_id=1, source_target_pairs={{3,0},{0,1},{1,2},{2,3},{7,4},{4,5},{5,6},{6,7},{11,8},{8,9},{9,10... | collective-permute-start | bytes 196616 | tf_op jit(solution)/shard_map/ppermute | solution.py:20
  89.3 9.3 %collective-permute-start.19 = (bf16[64,512]{1,0:T(8,128)(2,1)S(1)}, bf16[64,512]{1,0:T(8,128)(2,1)S(1)}, u32[]{:S(2)}, u32[]{:S(2)}) collective-permute-start(bf16[64,512]{1,0:T(8,128)(2,1)S(1)} %get-tuple-element.36), channel_id=1, source_target_pairs={{2,0},{3,1},{0,2},{1,3},{6,4},{7,5},{4,6},{5,7},{10,8},{11,9},{8,1... | collective-permute-start | bytes 196616 | tf_op jit(solution)/shard_map/ppermute | solution.py:20
  90.8 7.7 %collective-permute-start.18 = (bf16[64,512]{1,0:T(8,128)(2,1)S(1)}, bf16[64,512]{1,0:T(8,128)(2,1)S(1)}, u32[]{:S(2)}, u32[]{:S(2)}) collective-permute-start(bf16[64,512]{1,0:T(8,128)(2,1)S(1)} %get-tuple-element.36), channel_id=1, source_target_pairs={{1,0},{2,1},{3,2},{0,3},{5,4},{6,5},{7,6},{4,7},{9,8},{10,9},{11,1... | collective-permute-start | bytes 196616 | tf_op jit(solution)/shard_map/ppermute | solution.py:20
  94.7 11.9 %all-to-all-start.1 = ((bf16[4,64,1024]{2,1,0:T(8,128)(2,1)}), bf16[4,64,1024]{2,1,0:T(8,128)(2,1)S(1)}, u32[]{:S(2)}, u32[]{:S(2)}) async-start(bf16[4,64,1024]{2,1,0:T(8,128)(2,1)} %broadcast_in_dim.9), calls=%async_computation.1 | async-start | bytes 1048576 | tf_op jit(solution)/shard_map/all_to_all | solution.py:29
  98.6 9.6 %collective-permute-start.23 = (bf16[256,512]{1,0:T(8,128)(2,1)S(1)}, bf16[256,512]{1,0:T(8,128)(2,1)}, u32[]{:S(2)}, u32[]{:S(2)}) collective-permute-start(bf16[256,512]{1,0:T(8,128)(2,1)S(1)} %pad_maximum_fusion.2), channel_id=1, source_target_pairs={{192,0},{0,64},{64,128},{128,192},{193,1},{1,65},{65,129},{129,193... | collective-permute-start | bytes 786440 | tf_op jit(solution)/shard_map/ppermute | solution.py:20
  99.9 11.1 %collective-permute-start.22 = (bf16[256,512]{1,0:T(8,128)(2,1)S(1)}, bf16[256,512]{1,0:T(8,128)(2,1)}, u32[]{:S(2)}, u32[]{:S(2)}) collective-permute-start(bf16[256,512]{1,0:T(8,128)(2,1)S(1)} %pad_maximum_fusion.2), channel_id=1, source_target_pairs={{128,0},{192,64},{0,128},{64,192},{129,1},{193,65},{1,129},{65,193... | collective-permute-start | bytes 786440 | tf_op jit(solution)/shard_map/ppermute | solution.py:20
  102.3 8.9 %collective-permute-start.21 = (bf16[256,512]{1,0:T(8,128)(2,1)S(1)}, bf16[256,512]{1,0:T(8,128)(2,1)}, u32[]{:S(2)}, u32[]{:S(2)}) collective-permute-start(bf16[256,512]{1,0:T(8,128)(2,1)S(1)} %pad_maximum_fusion.2), channel_id=1, source_target_pairs={{64,0},{128,64},{192,128},{0,192},{65,1},{129,65},{193,129},{1,193... | collective-permute-start | bytes 786440 | tf_op jit(solution)/shard_map/ppermute | solution.py:20
  113.1 1.5 copy-start.3
  114.6 1.3 copy-start.5
  115.8 1.9 copy-start.6
  115.8 2.0 copy-start.21
  115.8 2.8 %copy-start.7 = (bf16[1792,512]{1,0:T(8,128)(2,1)S(1)}, bf16[1792,512]{1,0:T(8,128)(2,1)}, u32[]{:S(2)}) copy-start(bf16[1792,512]{1,0:T(8,128)(2,1)} %param.26) | copy-start | bytes 5505028
  117.7 1.8 copy-start.13
  117.7 1.8 copy-start.15
  117.7 1.9 copy-start.11
  117.7 1.9 copy-start.10
  117.7 11.5 %collective-permute-start.24 = (f32[128,3584]{1,0:T(8,128)}, f32[128,3584]{1,0:T(8,128)}, u32[]{:S(2)}, u32[]{:S(2)}) collective-permute-start(f32[128,3584]{1,0:T(8,128)} %pad_maximum_fusion), channel_id=1, source_target_pairs={{0,8},{8,0},{1,9},{9,1},{2,10},{10,2},{3,11},{11,3},{4,12},{12,4},... | collective-permute-start | bytes 5505032 | tf_op jit(solution)/shard_map/ppermute | solution.py:24
  119.4 3.7 %collective-permute-start.17 = (f32[128,1792]{1,0:T(8,128)S(1)}, f32[128,1792]{1,0:T(8,128)S(1)}, u32[]{:S(2)}, u32[]{:S(2)}) collective-permute-start(f32[128,1792]{1,0:T(8,128)S(1)} %fusion.42), channel_id=1, source_target_pairs={{0,8},{8,0},{1,9},{9,1},{2,10},{10,2},{3,11},{11,3},{4,12},{12,4},... | collective-permute-start | bytes 2752520 | tf_op jit(solution)/shard_map/ppermute | solution.py:24
  124.6 20.8 %all-to-all-start.2 = ((bf16[4,32,1792]{2,1,0:T(8,128)(2,1)}), bf16[4,32,1792]{2,1,0:T(8,128)(2,1)S(1)}, u32[]{:S(2)}, u32[]{:S(2)}) async-start(bf16[4,32,1792]{2,1,0:T(8,128)(2,1)} %bitcast.7), calls=%async_computation.2 | async-start | bytes 917504 | tf_op jit(solution)/shard_map/all_to_all | solution.py:390
  129.1 10.5 %copy-start.9 = (s32[256]{0:T(256)S(1)}, s32[256]{0:T(256)}, u32[]{:S(2)}) copy-start(s32[256]{0:T(256)} %get-tuple-element.26) | copy-start | bytes 3076
  133.4 23.4 %collective-permute-start.25 = (bf16[32,3584]{1,0:T(8,128)(2,1)}, bf16[32,3584]{1,0:T(8,128)(2,1)S(1)}, u32[]{:S(2)}, u32[]{:S(2)}) collective-permute-start(bf16[32,3584]{1,0:T(8,128)(2,1)} %get-tuple-element.39), channel_id=1, source_target_pairs={{16,0},{32,16},{48,32},{0,48},{17,1},{33,17},{49,33},{1,49},{18,2}... | collective-permute-start | bytes 688136 | tf_op jit(solution)/shard_map/ppermute | solution.py:20
  133.4 23.4 %collective-permute-start.27 = (bf16[32,3584]{1,0:T(8,128)(2,1)}, bf16[32,3584]{1,0:T(8,128)(2,1)S(1)}, u32[]{:S(2)}, u32[]{:S(2)}) collective-permute-start(bf16[32,3584]{1,0:T(8,128)(2,1)} %get-tuple-element.40), channel_id=1, source_target_pairs={{48,0},{0,16},{16,32},{32,48},{49,1},{1,17},{17,33},{33,49},{50,2}... | collective-permute-start | bytes 688136 | tf_op jit(solution)/shard_map/ppermute | solution.py:20
  135.5 23.4 %collective-permute-start.26 = (bf16[32,3584]{1,0:T(8,128)(2,1)S(1)}, bf16[32,3584]{1,0:T(8,128)(2,1)S(1)}, u32[]{:S(2)}, u32[]{:S(2)}) collective-permute-start(bf16[32,3584]{1,0:T(8,128)(2,1)S(1)} %get-tuple-element.41), channel_id=1, source_target_pairs={{32,0},{48,16},{0,32},{16,48},{33,1},{49,17},{1,33},{17,49},{34,2}... | collective-permute-start | bytes 688136 | tf_op jit(solution)/shard_map/ppermute | solution.py:20
  139.6 26.3 %copy-start.8 = (s32[256]{0:T(256)S(1)}, s32[256]{0:T(256)}, u32[]{:S(2)}) copy-start(s32[256]{0:T(256)} %get-tuple-element.27) | copy-start | bytes 3076
  160.2 9.9 %collective-permute-start.30 = (bf16[32,3584]{1,0:T(8,128)(2,1)S(1)}, bf16[32,3584]{1,0:T(8,128)(2,1)S(1)}, u32[]{:S(2)}, u32[]{:S(2)}) collective-permute-start(bf16[32,3584]{1,0:T(8,128)(2,1)S(1)} %pad_maximum_fusion.4), channel_id=1, source_target_pairs={{48,0},{0,16},{16,32},{32,48},{49,1},{1,17},{17,33},{33,49},{50,2}... | collective-permute-start | bytes 688136 | tf_op jit(solution)/shard_map/ppermute | solution.py:20
  161.7 18.9 %collective-permute-start.29 = (bf16[32,3584]{1,0:T(8,128)(2,1)S(1)}, bf16[32,3584]{1,0:T(8,128)(2,1)S(1)}, u32[]{:S(2)}, u32[]{:S(2)}) collective-permute-start(bf16[32,3584]{1,0:T(8,128)(2,1)S(1)} %pad_maximum_fusion.4), channel_id=1, source_target_pairs={{32,0},{48,16},{0,32},{16,48},{33,1},{49,17},{1,33},{17,49},{34,2}... | collective-permute-start | bytes 688136 | tf_op jit(solution)/shard_map/ppermute | solution.py:20
  165.9 18.6 %collective-permute-start.28 = (bf16[32,3584]{1,0:T(8,128)(2,1)S(1)}, bf16[32,3584]{1,0:T(8,128)(2,1)S(1)}, u32[]{:S(2)}, u32[]{:S(2)}) collective-permute-start(bf16[32,3584]{1,0:T(8,128)(2,1)S(1)} %pad_maximum_fusion.4), channel_id=1, source_target_pairs={{16,0},{32,16},{48,32},{0,48},{17,1},{33,17},{49,33},{1,49},{18,2}... | collective-permute-start | bytes 688136 | tf_op jit(solution)/shard_map/ppermute | solution.py:20
  166.0 19.5 %copy-start.4 = (bf16[512,1792]{1,0:T(8,128)(2,1)S(1)}, bf16[512,1792]{1,0:T(8,128)(2,1)}, u32[]{:S(2)}) copy-start(bf16[512,1792]{1,0:T(8,128)(2,1)} %param.24) | copy-start | bytes 5505028
  184.6 2.6 %collective-permute-start.31 = (bf16[128,3584]{1,0:T(8,128)(2,1)S(1)}, bf16[128,3584]{1,0:T(8,128)(2,1)S(1)}, u32[]{:S(2)}, u32[]{:S(2)}) collective-permute-start(bf16[128,3584]{1,0:T(8,128)(2,1)S(1)} %pad_maximum_fusion.1), channel_id=1, source_target_pairs={{0,8},{8,0},{1,9},{9,1},{2,10},{10,2},{3,11},{11,3},{4,12},{12,4},... | collective-permute-start | bytes 2752520 | tf_op jit(solution)/shard_map/ppermute | solution.py:24
  188.9 9.6 %collective-permute-start.34 = (bf16[256,512]{1,0:T(8,128)(2,1)S(1)}, bf16[256,512]{1,0:T(8,128)(2,1)S(1)}, u32[]{:S(2)}, u32[]{:S(2)}) collective-permute-start(bf16[256,512]{1,0:T(8,128)(2,1)S(1)} %convolution_convert_fusion), channel_id=1, source_target_pairs={{192,0},{0,64},{64,128},{128,192},{193,1},{1,65},{65,129},{129,193... | collective-permute-start | bytes 786440 | tf_op jit(solution)/shard_map/ppermute | solution.py:20
  190.9 9.3 %collective-permute-start.33 = (bf16[256,512]{1,0:T(8,128)(2,1)S(1)}, bf16[256,512]{1,0:T(8,128)(2,1)S(1)}, u32[]{:S(2)}, u32[]{:S(2)}) collective-permute-start(bf16[256,512]{1,0:T(8,128)(2,1)S(1)} %convolution_convert_fusion.1), channel_id=1, source_target_pairs={{64,0},{128,64},{192,128},{0,192},{65,1},{129,65},{193,129},{1,193... | collective-permute-start | bytes 786440 | tf_op jit(solution)/shard_map/ppermute | solution.py:20
  192.8 12.2 %collective-permute-start.32 = (bf16[256,512]{1,0:T(8,128)(2,1)S(1)}, bf16[256,512]{1,0:T(8,128)(2,1)S(1)}, u32[]{:S(2)}, u32[]{:S(2)}) collective-permute-start(bf16[256,512]{1,0:T(8,128)(2,1)S(1)} %convolution_convert_fusion.2), channel_id=1, source_target_pairs={{128,0},{192,64},{0,128},{64,192},{129,1},{193,65},{1,129},{65,193... | collective-permute-start | bytes 786440 | tf_op jit(solution)/shard_map/ppermute | solution.py:20
  205.3 7.4 %collective-permute-start.35 = (bf16[128,512]{1,0:T(8,128)(2,1)S(1)}, bf16[128,512]{1,0:T(8,128)(2,1)S(1)}, u32[]{:S(2)}, u32[]{:S(2)}) collective-permute-start(bf16[128,512]{1,0:T(8,128)(2,1)S(1)} %pad_maximum_fusion.6), channel_id=1, source_target_pairs={{2,0},{3,1},{0,2},{1,3},{6,4},{7,5},{4,6},{5,7},{10,8},{11,9},{8,1... | collective-permute-start | bytes 393224 | tf_op jit(solution)/shard_map/ppermute | solution.py:20
  208.7 6.0 %collective-permute-start.36 = (bf16[128,512]{1,0:T(8,128)(2,1)S(1)}, bf16[128,512]{1,0:T(8,128)(2,1)S(1)}, u32[]{:S(2)}, u32[]{:S(2)}) collective-permute-start(bf16[128,512]{1,0:T(8,128)(2,1)S(1)} %pad_maximum_fusion.7), channel_id=1, source_target_pairs={{1,0},{2,1},{3,2},{0,3},{5,4},{6,5},{7,6},{4,7},{9,8},{10,9},{11,1... | collective-permute-start | bytes 393224 | tf_op jit(solution)/shard_map/ppermute | solution.py:20
  209.9 6.3 %collective-permute-start.37 = (bf16[128,512]{1,0:T(8,128)(2,1)S(1)}, bf16[128,512]{1,0:T(8,128)(2,1)S(1)}, u32[]{:S(2)}, u32[]{:S(2)}) collective-permute-start(bf16[128,512]{1,0:T(8,128)(2,1)S(1)} %pad_maximum_fusion.8), channel_id=1, source_target_pairs={{3,0},{0,1},{1,2},{2,3},{7,4},{4,5},{5,6},{6,7},{11,8},{8,9},{9,10... | collective-permute-start | bytes 393224 | tf_op jit(solution)/shard_map/ppermute | solution.py:20
  216.3 8.3 %collective-permute-start.38 = (bf16[2,32,512]{2,1,0:T(8,128)(2,1)S(1)}, bf16[2,32,512]{2,1,0:T(8,128)(2,1)S(1)}, u32[]{:S(2)}, u32[]{:S(2)}) collective-permute-start(bf16[2,32,512]{2,1,0:T(8,128)(2,1)S(1)} %fusion.63), channel_id=1, source_target_pairs={{0,4},{4,0},{1,5},{5,1},{2,6},{6,2},{3,7},{7,3},{8,12},{12,8},{9,1... | collective-permute-start | bytes 196616 | tf_op jit(solution)/shard_map/ppermute | solution.py:24
where the time goes:
time: 226 us; the launch traced here: 225 us
  waiting for transfers between devices  106 us (47%)
  starting transfers between devices  74.1 us (33%)
  local copies, waits for them, and re-layouts  14.7 us (7%)
  other arithmetic  13.2 us (6%)
  matrix products  9.81 us (4%)
  Pallas kernels  6.07 us (3%)
    ppermute x30, waiting for transfers between devices, from_next(): return lax.ppermute(value, axis, [((i + k) % n, i) for i in range(n)])  70.6 us
    ppermute x30, starting transfers between devices, from_next(): return lax.ppermute(value, axis, [((i + k) % n, i) for i in range(n)])  51.8 us
    ppermute x9, waiting for transfers between devices, swap(): return lax.ppermute(value, axis, [(0, 1), (1, 0)])  20.6 us
    ppermute x9, starting transfers between devices, swap(): return lax.ppermute(value, axis, [(0, 1), (1, 0)])  9.39 us
    unnamed x53, local copies, waits for them, and re-layouts  8.83 us
    all_to_all x1, waiting for transfers between devices, local(): lax.all_to_all(pair_sum(keep, near), 'zl', 0, 0, tiled=True).astype(F32)  6.39 us
    all_to_all x1, waiting for transfers between devices, local(): lax.all_to_all(near, 'zl', 0, 0, tiled=True).astype(F32)  5.71 us
    dot_general x6, matrix products, mm_t(): lax.dot_general(a, b, (((1,), (1,)), ((), ())), preferred_element_type=F32)  5.08 us
  transfers between devices with their start and end apart: 42, of which 31 were waited for; matrix products, arithmetic and copies ran while one was open for 11% of the time, Pallas kernels for 3%

commit v1 on v0

--- a/solution.py
+++ b/solution.py
@@ -113,35 +113,24 @@
 
 
 def first_kernel(
-    c_ref, x0, x1, x2, x3, gain_ref, bias_ref, w0, w1, w2, w3,
-    keep_ref, send_ref, out_ref, shift_ref, z_ref, w_ref, extra_ref, sems
+    c_ref, x0, x1, x2, x3, gain_ref, bias_ref, w0, w1, w2, w3, keep_ref, send_ref, z_ref, w_ref, sems
 ):
     n, feats = x0.shape
     count = 4 * n
     units = w0.shape[1]
     half = 2 * units
-    copies = []
-
-    def copy(src, dst):
-        copies.append(pltpu.make_async_copy(src, dst, sems.at[len(copies)]))
-        copies[-1].start()
-
-    ws = (w0, w1, w2, w3)
-    for k, w in enumerate(ws):
-        copy(w.at[pl.ds(0, feats)], w_ref.at[:, pl.ds(k * units, units)])
-    for k, w in enumerate(ws):
-        for j in range(out_ref.shape[1] // units):
-            copy(
-                w.at[pl.ds(feats + j * units, units)],
-                out_ref.at[pl.ds(k * units, units), pl.ds(j * units, units)],
-            )
-        copy(w.at[pl.ds(w.shape[0] - 16, 16)], extra_ref.at[:, pl.ds(k * units, units)])
+    copies = [
+        pltpu.make_async_copy(w, w_ref.at[:, pl.ds(k * units, units)], sems.at[k])
+        for k, w in enumerate((w0, w1, w2, w3))
+    ]
+    for copy in copies:
+        copy.start()
     gain = gain_ref[...]
-    step = 16
+    step = n // 4
     lane = lax.broadcasted_iota(jnp.int32, (step, units), 1)
     for k, x_ref in enumerate((x0, x1, x2, x3)):
 
-        @pl.loop(0, n // step)
+        @pl.loop(0, 4)
         def _(i):
             x = x_ref[pl.ds(pl.multiple_of(i * step, step), step), :].astype(F32)
             mean = jnp.sum(x, axis=1, keepdims=True) * (1.0 / feats)
@@ -155,44 +144,43 @@
 
     extra = []
     for v in (gain, bias_ref[...]):
-        extra += pieces(v)
+        for _ in range(3):
+            part = v.astype(BF).astype(F32)
+            extra.append(part)
+            v = v - part
     extra.append(jnp.zeros((10, feats), F32))
     z_ref[count:, :] = jnp.concatenate(extra, axis=0).astype(BF)
     for ref in (keep_ref, send_ref):
         ref[count:, half:] = jnp.zeros((16, units), F32)
-    for one in copies:
-        one.wait()
+    for copy in copies:
+        copy.wait()
     p = jnp.dot(z_ref[...], w_ref[...], preferred_element_type=F32)
     low = c_ref[0] == 0
     keep_ref[:, :half] = jnp.where(low, p[:, :half], p[:, half:])
     send_ref[:, :half] = jnp.where(low, p[:, half:], p[:, :half])
-    shift = jnp.sum(extra_ref[...].astype(F32), axis=0, keepdims=True)
-    shift_ref[...] = jnp.where(low, shift[:, :half], shift[:, half:])
-
-
-def first_layer(rows, gain, bias, w_all, c_ref, cols):
+
+
+def first_layer(rows, gain, bias, w_in, c_ref):
     n, feats = rows[0].shape
     count = 4 * n
-    units = w_all[0].shape[1]
+    units = w_in[0].shape[1]
     shape = (count + 16, 3 * units)
     return pl.pallas_call(
         first_kernel,
-        out_shape=[jax.ShapeDtypeStruct(shape, F32)] * 2
-        + [jax.ShapeDtypeStruct((4 * units, cols), BF), jax.ShapeDtypeStruct((1, 2 * units), F32)],
+        out_shape=[jax.ShapeDtypeStruct(shape, F32)] * 2,
         in_specs=[SMEM] + [VMEM] * 6 + [ANY] * 4,
-        out_specs=[VMEM] * 4,
+        out_specs=[VMEM, VMEM],
         scratch_shapes=[
             pltpu.VMEM((count + 16, feats), BF),
             pltpu.VMEM((feats, 4 * units), BF),
-            pltpu.VMEM((16, 4 * units), BF),
-            pltpu.SemaphoreType.DMA((8 + 4 * (cols // units),)),
+            pltpu.SemaphoreType.DMA((4,)),
         ],
         compiler_params=pltpu.CompilerParams(vmem_limit_bytes=32 << 20),
         cost_estimate=pl.CostEstimate(
             flops=2 * count * feats * 4 * units, bytes_accessed=4 << 20, transcendentals=0
         ),
         name="first_layer",
-    )(c_ref, *rows, gain.reshape(1, -1), bias.reshape(1, -1), *w_all)
+    )(c_ref, *rows, gain.reshape(1, -1), bias.reshape(1, -1), *w_in)
 
 
 def pieces(v):
@@ -255,21 +243,22 @@
 
 def second_kernel(c_ref, at_ref, own_ref, other_ref, w_ref, kept, s1, s2, s3, sum_ref):
     n = kept.shape[0]
-    half = own_ref.shape[1]
+    units = w_ref.shape[1] - 16
     low = c_ref[0] == 0
-    own, other = own_ref[...].astype(F32), other_ref[...].astype(F32)
-    first = jnp.where(low, own, other).astype(BF)
-    last = jnp.where(low, other, own).astype(BF)
-    sum_ref[...] = jnp.dot(
-        first, w_ref[:half, :], preferred_element_type=F32
-    ) + jnp.dot(last, w_ref[half:, :], preferred_element_type=F32)
+    total = jnp.zeros(sum_ref.shape, F32)
+    for j in range(4):
+        at = slice((j % 2) * units, (j % 2 + 1) * units)
+        a, b = (own_ref, other_ref) if j < 2 else (other_ref, own_ref)
+        act = jnp.where(low, a[:, at].astype(F32), b[:, at].astype(F32)).astype(BF)
+        total += jnp.dot(act, w_ref[at_ref[4 + j], :units, :], preferred_element_type=F32)
+    sum_ref[...] = total
     for k, ref in enumerate((kept, s1, s2, s3)):
         ref[...] = sum_ref[pl.ds(pl.multiple_of(at_ref[k], n), n), :].astype(ref.dtype)
 
 
 def second_layer(own, other, w_out, c_ref, at):
     count = own.shape[0]
-    cols = w_out.shape[1]
+    cols = w_out.shape[2]
     out = (count // 4, cols)
     return pl.pallas_call(
         second_kernel,
@@ -308,13 +297,11 @@
     cols = text_rows.shape[1]
 
     patch_other = swap(patches, "zh")
+    w_in = [proj_in] + [from_next(proj_in, "g", k) for k in (1, 2, 3)]
     packed = jnp.concatenate(
-        [proj_in]
-        + [proj_out[:, k * units : (k + 1) * units] for k in range(cols // units)]
-        + [jnp.pad(three_parts(proj_in_bias), ((0, 13), (0, 0)))],
-        axis=0,
-    )
-    w_all = line_of(packed, "g")
+        [proj_out, jnp.pad(three_parts(proj_in_bias), ((0, 13), (0, cols - units)))], axis=0
+    )
+    w_out = copy_for_each(packed, "g")
     pair = in_order(patches, patch_other, zh)
     rows = line_of(pair, "x")
     own = patches.shape[0]
@@ -323,15 +310,20 @@
     side = jnp.concatenate([text_rows, out_grads], axis=1)
     side_other = swap(side, "zh")
     side_pair = in_order(side, side_other, zh)
-    side_all = copy_for_each(side_pair, "x").reshape(count, 2 * cols)
+    side_all = jnp.concatenate(line_of(side_pair, "x"), axis=0)
     text, cotangent = side_all[:, :cols], side_all[:, cols:]
 
     half = 2 * units
     c_ref = c.reshape(1).astype(jnp.int32)
-    keep, send, w_out, bias = first_layer(rows, norm_gain, norm_bias, w_all, c_ref, cols)
+    keep, send = first_layer(rows, norm_gain, norm_bias, w_in, c_ref)
     near = swap(send, "c")
     turns = jnp.arange(4, dtype=jnp.int32)
     n = 2 * own
+    order = (g + turns) % 4
+    bias = jnp.sum(w_out[:, units : units + 3, :units].astype(F32), axis=1)
+    bias = jnp.where((order[:, None] == turns[None, :])[:, :, None], bias[None], 0.0)
+    bias = lax.optimization_barrier(jnp.sum(bias, axis=1).reshape(-1))
+    bias = jnp.where(c == 0, bias[:half], bias[half:])
     parts = lax.all_to_all(pair_sum(keep, near), "zl", 0, 0, tiled=True).astype(F32)
     means = jnp.sum(parts[:, :n, half : half + 3], axis=2, keepdims=True)
     spreads = jnp.sum(parts[:, :n, half + 3 : half + 6], axis=2, keepdims=True)
@@ -340,12 +332,12 @@
     mean = jnp.mean(means, axis=0, keepdims=True)
     spread = jnp.mean(spreads + (means - mean) * (means - mean), axis=0)
     total = jnp.sum(parts[:, :n, :half] + (means - mean) * gains, axis=0)
-    total = total * lax.rsqrt(spread + 1e-05) + (shift + bias[0])
+    total = total * lax.rsqrt(spread + 1e-05) + (shift + bias)
     activated = jax.nn.gelu(total, approximate=False).astype(BF)
-    act_own = jnp.concatenate(line_of(activated, "zl"), axis=0)
+    act_own = copy_for_each(activated, "zl").reshape(count, half)
     act_other = swap(act_own, "c")
 
-    part, *sent = second_layer(act_own, act_other, w_out, c_ref, (-turns - zl) % 4 * n)
+    part, *sent = second_layer(act_own, act_other, w_out, c_ref, jnp.concatenate([-turns % 4 * n, order]))
     for k, v in enumerate(sent):
         part = part + from_next(v, "x", k + 1).astype(F32)
     part = part + swap(part.astype(BF), "zh").astype(F32)
@@ -367,10 +359,11 @@
     def x_turned(p):
         return (p - x * (2 * own)) % count
 
+    text_place = x_turned(place)
     column = jnp.where(
         covered,
         (source // count - g) % 4 * count + x_turned(gathered_place(source % count)),
-        4 * count + place,
+        4 * count + text_place,
     )
     column = lax.optimization_barrier(column)
     choose = column[:, None]
@@ -380,7 +373,8 @@
     far_inputs = mm(far_choice.astype(BF), jnp.concatenate(far_rows, axis=0))
     inputs = (near_inputs + far_inputs).astype(BF)
     z_block = q // own % 4 * 2 + (c + q // (4 * own)) % 2
-    reorder = (gathered_place(z_block * own + q % own)[:, None] == q[None, :]).astype(BF)
+    reorder = x_turned(gathered_place(z_block * own + q % own))
+    reorder = (reorder[:, None] == q[None, :]).astype(BF)
     back_rows = pick(reorder, cotangent)
 
     given = mm_t(back_rows[4 * own :], down_weight)

time: 226 us -> 221 us (0.978)
  local copies, waits for them, and re-layouts: 14.7 us -> 6.23 us
  starting transfers between devices: 74.1 us -> 80.1 us
    unnamed x53 -> x44, local copies, waits for them, and re-layouts: 8.83 us -> 2.55 us
    ppermute x9, waiting for transfers between devices: 20.6 us -> 14.4 us  [swap(): return lax.ppermute(value, axis, [(0, 1), (1, 0)])]
    all_to_all x1 -> x2, starting transfers between devices: 3.78 us -> 8.7 us  [copy_for_each(): lax.all_to_all(jnp.broadcast_to(shard[None], (count, *shard.shape)), axis...]
    ppermute x9, starting transfers between devices: 9.39 us -> 12.1 us  [swap(): return lax.ppermute(value, axis, [(0, 1), (1, 0)])]
    all_to_all x1 -> x2, waiting for transfers between devices: 2.73 us -> 5.02 us  [copy_for_each(): lax.all_to_all(jnp.broadcast_to(shard[None], (count, *shard.shape)), axis...]
  transfers between devices with their start and end apart: 42 -> 43, of which waited for: 31 -> 30; matrix products, arithmetic and copies ran while one was open for 11% -> 9% of each run, Pallas kernels for 3% -> 3%
where the time goes in v1:
time: 221 us; the launch traced here: 220 us
  waiting for transfers between devices  104 us (47%)
  starting transfers between devices  80.1 us (36%)
  other arithmetic  13.9 us (6%)
  matrix products  8.67 us (4%)
  local copies, waits for them, and re-layouts  6.23 us (3%)
  Pallas kernels  5.92 us (3%)
    ppermute x30, waiting for transfers between devices, from_next(): return lax.ppermute(value, axis, [((i + k) % n, i) for i in range(n)])  71.6 us
    ppermute x30, starting transfers between devices, from_next(): return lax.ppermute(value, axis, [((i + k) % n, i) for i in range(n)])  51.5 us
    ppermute x9, waiting for transfers between devices, swap(): return lax.ppermute(value, axis, [(0, 1), (1, 0)])  14.4 us
    ppermute x9, starting transfers between devices, swap(): return lax.ppermute(value, axis, [(0, 1), (1, 0)])  12.1 us
    all_to_all x2, starting transfers between devices, copy_for_each(): lax.all_to_all(jnp.broadcast_to(shard[None], (count, *shard.shape)), axis...  8.7 us
    all_to_all x1, waiting for transfers between devices, local(): lax.all_to_all(pair_sum(keep, near), 'zl', 0, 0, tiled=True).astype(F32)  7.09 us
    all_to_all x1, waiting for transfers between devices, local(): lax.all_to_all(near, 'zl', 0, 0, tiled=True).astype(F32)  5.69 us
    dot_general x6, matrix products, mm_t(): lax.dot_general(a, b, (((1,), (1,)), ((), ())), preferred_element_type=F32)  5.06 us
  transfers between devices with their start and end apart: 43, of which 30 were waited for; matrix products, arithmetic and copies ran while one was open for 9% of the time, Pallas kernels for 3%

profile of v1, /device:TPU:32, one launch (start us, length us, event | category | flops | bytes accessed | tf_op | source)
XLA Modules:
  0.0 220.0 jit_solution(10642779699663657111)
XLA Ops:
  0.7 3.3 %collective-permute-start.5 = (bf16[1600,128]{1,0:T(8,128)(2,1)}, bf16[1600,128]{1,0:T(8,128)(2,1)S(1)}, u32[]{:S(2)}, u32[]{:S(2)}) collective-permute-start(bf16[1600,128]{1,0:T(8,128)(2,1)} %w0.1), channel_id=1, source_target_pairs={{128,0},{192,64},{0,128},{64,192},{129,1},{193,65},{1,129},{65,193... | collective-permute-start | bytes 1228808 | tf_op jit(solution)/shard_map/ppermute | solution.py:20
  4.0 1.1 collective-permute-start.4
  5.0 1.0 collective-permute-start.6
  6.0 6.3 %collective-permute-start = (bf16[32,1600]{1,0:T(8,128)(2,1)}, bf16[32,1600]{1,0:T(8,128)(2,1)S(1)}, u32[]{:S(2)}, u32[]{:S(2)}) collective-permute-start(bf16[32,1600]{1,0:T(8,128)(2,1)} %param.15), channel_id=1, source_target_pairs={{0,4},{4,0},{1,5},{5,1},{2,6},{6,2},{3,7},{7,3},{8,12},{12,8},{9,1... | collective-permute-start | bytes 307208 | tf_op jit(solution)/shard_map/ppermute | solution.py:24
  13.0 0.9 pad_maximum_fusion.6
  14.8 3.5 %all-to-all-start.1 = ((bf16[4,144,512]{2,1,0:T(8,128)(2,1)}), bf16[4,144,512]{2,1,0:T(8,128)(2,1)S(1)}, u32[]{:S(2)}, u32[]{:S(2)}) async-start(bf16[4,144,512]{2,1,0:T(8,128)(2,1)} %broadcast_in_dim.32), calls=%async_computation.1 | async-start | bytes 1179648 | tf_op jit(solution)/shard_map/all_to_all | solution.py:29
  20.5 1.4 select_reduce_fusion.3
  22.0 1.6 collective-permute-start.3
  23.6 2.8 %collective-permute-start.2 = (bf16[64,1600]{1,0:T(8,128)(2,1)S(1)}, bf16[64,1600]{1,0:T(8,128)(2,1)S(1)}, u32[]{:S(2)}, u32[]{:S(2)}) collective-permute-start(bf16[64,1600]{1,0:T(8,128)(2,1)S(1)} %maximum_select_fusion.x0), channel_id=1, source_target_pairs={{2,0},{3,1},{0,2},{1,3},{6,4},{7,5},{4,6},{5,7},{10,8},{11,9},{8,1... | collective-permute-start | bytes 614408 | tf_op jit(solution)/shard_map/ppermute | solution.py:20
  26.4 4.0 %collective-permute-done.3.x3 = bf16[64,1600]{1,0:T(8,128)(2,1)S(1)} collective-permute-done((bf16[64,1600]{1,0:T(8,128)(2,1)S(1)}, bf16[64,1600]{1,0:T(8,128)(2,1)S(1)}, u32[]{:S(2)}, u32[]{:S(2)}) %collective-permute-start.3) | collective-permute-done | bytes 204832 | tf_op jit(solution)/shard_map/ppermute | solution.py:20
  30.4 2.5 %collective-permute-start.1 = (bf16[64,1600]{1,0:T(8,128)(2,1)S(1)}, bf16[64,1600]{1,0:T(8,128)(2,1)S(1)}, u32[]{:S(2)}, u32[]{:S(2)}) collective-permute-start(bf16[64,1600]{1,0:T(8,128)(2,1)S(1)} %maximum_select_fusion.x0), channel_id=1, source_target_pairs={{1,0},{2,1},{3,2},{0,3},{5,4},{6,5},{7,6},{4,7},{9,8},{10,9},{11,1... | collective-permute-start | bytes 614408 | tf_op jit(solution)/shard_map/ppermute | solution.py:20
  33.7 1.0 collective-permute-done.2.x2
  35.0 1.3 collective-permute-done.1.x1
  36.3 4.0 %first_layer.1 = (f32[272,384]{1,0:T(8,128)S(1)}, f32[272,384]{1,0:T(8,128)S(1)}) custom-call(s32[1]{0:T(128)} %bitcast.c_ref, bf16[64,1600]{1,0:T(8,128)(2,1)S(1)} %maximum_select_fusion.x0, bf16[64,1600]{1,0:T(8,128)(2,1)S(1)} %collective-permute-done.1.x1, bf16[64,1600]{1,0:T(8,128)(2,1)S(1)} %collective-permute-done.2.x2, ...), custom_call_target="tpu_custom_call" | custom-call | flops 419430400 | bytes 4194304 | tf_op jit(solution)/shard_map/first_layer/pallas_call | solution.py:168
  40.5 1.6 collective-permute-done.7.near_ref
  42.1 1.0 pair_sum.1
  43.1 4.4 %all-to-all-start = ((bf16[4,80,384]{2,1,0:T(8,128)(2,1)}), bf16[4,80,384]{2,1,0:T(8,128)(2,1)S(1)}, u32[]{:S(2)}, u32[]{:S(2)}) async-start(bf16[4,80,384]{2,1,0:T(8,128)(2,1)} %pair_sum.1), calls=%async_computation | async-start | bytes 491520 | tf_op jit(solution)/shard_map/all_to_all | solution.py:327
  47.6 7.1 %all-to-all-done = bf16[4,80,384]{2,1,0:T(8,128)(2,1)S(1)} async-done(((bf16[4,80,384]{2,1,0:T(8,128)(2,1)}), bf16[4,80,384]{2,1,0:T(8,128)(2,1)S(1)}, u32[]{:S(2)}, u32[]{:S(2)}) %all-to-all-start) | async-done | bytes 245792 | tf_op jit(solution)/shard_map/all_to_all | solution.py:327
  56.1 5.2 %all-to-all-start.2 = ((bf16[4,64,256]{2,1,0:T(8,128)(2,1)}), bf16[4,64,256]{2,1,0:T(8,128)(2,1)S(1)}, u32[]{:S(2)}, u32[]{:S(2)}) async-start(bf16[4,64,256]{2,1,0:T(8,128)(2,1)} %broadcast_in_dim.35), calls=%async_computation.2 | async-start | bytes 262144 | tf_op jit(solution)/shard_map/all_to_all | solution.py:29
  61.4 5.0 %all-to-all-done.2 = bf16[4,64,256]{2,1,0:T(8,128)(2,1)S(1)} async-done(((bf16[4,64,256]{2,1,0:T(8,128)(2,1)}), bf16[4,64,256]{2,1,0:T(8,128)(2,1)S(1)}, u32[]{:S(2)}, u32[]{:S(2)}) %all-to-all-start.2) | async-done | bytes 131104 | tf_op jit(solution)/shard_map/all_to_all | solution.py:29
  66.5 1.3 collective-permute-done.8.other_ref
  67.8 1.0 second_layer.1
  68.8 3.8 %collective-permute-start.9 = (bf16[64,512]{1,0:T(8,128)(2,1)S(1)}, bf16[64,512]{1,0:T(8,128)(2,1)S(1)}, u32[]{:S(2)}, u32[]{:S(2)}) collective-permute-start(bf16[64,512]{1,0:T(8,128)(2,1)S(1)} %get-tuple-element.12), channel_id=1, source_target_pairs={{1,0},{2,1},{3,2},{0,3},{5,4},{6,5},{7,6},{4,7},{9,8},{10,9},{11,1... | collective-permute-start | bytes 196616 | tf_op jit(solution)/shard_map/ppermute | solution.py:20
  72.6 1.0 collective-permute-start.11
  73.6 2.1 collective-permute-done.9
  75.7 3.0 %collective-permute-done.10 = bf16[64,512]{1,0:T(8,128)(2,1)S(1)} collective-permute-done((bf16[64,512]{1,0:T(8,128)(2,1)S(1)}, bf16[64,512]{1,0:T(8,128)(2,1)S(1)}, u32[]{:S(2)}, u32[]{:S(2)}) %collective-permute-start.10) | collective-permute-done | bytes 65568 | tf_op jit(solution)/shard_map/ppermute | solution.py:20
  79.1 1.5 collective-permute-start.12
  81.4 2.6 %collective-permute-start.15 = (bf16[64,1024]{1,0:T(8,128)(2,1)S(1)}, bf16[64,1024]{1,0:T(8,128)(2,1)S(1)}, u32[]{:S(2)}, u32[]{:S(2)}) collective-permute-start(bf16[64,1024]{1,0:T(8,128)(2,1)S(1)} %maximum_select_fusion.1), channel_id=1, source_target_pairs={{2,0},{3,1},{0,2},{1,3},{6,4},{7,5},{4,6},{5,7},{10,8},{11,9},{8,1... | collective-permute-start | bytes 393224 | tf_op jit(solution)/shard_map/ppermute | solution.py:20
  84.6 3.3 %collective-permute-done.12 = bf16[64,512]{1,0:T(8,128)(2,1)S(1)} collective-permute-done((bf16[64,512]{1,0:T(8,128)(2,1)S(1)}, bf16[64,512]{1,0:T(8,128)(2,1)S(1)}, u32[]{:S(2)}, u32[]{:S(2)}) %collective-permute-start.12) | collective-permute-done | bytes 65568 | tf_op jit(solution)/shard_map/ppermute | solution.py:24
  88.0 2.5 %collective-permute-start.19 = (bf16[64,512]{1,0:T(8,128)(2,1)S(1)}, bf16[64,512]{1,0:T(8,128)(2,1)S(1)}, u32[]{:S(2)}, u32[]{:S(2)}) collective-permute-start(bf16[64,512]{1,0:T(8,128)(2,1)S(1)} %get-tuple-element.32), channel_id=1, source_target_pairs={{2,0},{3,1},{0,2},{1,3},{6,4},{7,5},{4,6},{5,7},{10,8},{11,9},{8,1... | collective-permute-start | bytes 196616 | tf_op jit(solution)/shard_map/ppermute | solution.py:20
  90.5 1.6 collective-permute-start.18
  92.2 2.0 collective-permute-done.20
  95.0 2.1 collective-permute-start.23
  97.1 2.7 %collective-permute-start.22 = (bf16[256,512]{1,0:T(8,128)(2,1)S(1)}, bf16[256,512]{1,0:T(8,128)(2,1)S(1)}, u32[]{:S(2)}, u32[]{:S(2)}) collective-permute-start(bf16[256,512]{1,0:T(8,128)(2,1)S(1)} %pad_maximum_fusion.3), channel_id=1, source_target_pairs={{128,0},{192,64},{0,128},{64,192},{129,1},{193,65},{1,129},{65,193... | collective-permute-start | bytes 786440 | tf_op jit(solution)/shard_map/ppermute | solution.py:20
  99.8 1.5 collective-permute-start.21
  101.3 3.7 %collective-permute-done.23 = bf16[256,512]{1,0:T(8,128)(2,1)S(1)} collective-permute-done((bf16[256,512]{1,0:T(8,128)(2,1)S(1)}, bf16[256,512]{1,0:T(8,128)(2,1)S(1)}, u32[]{:S(2)}, u32[]{:S(2)}) %collective-permute-start.23) | collective-permute-done | bytes 262176 | tf_op jit(solution)/shard_map/ppermute | solution.py:20
  105.0 4.5 %collective-permute-done.22 = bf16[256,512]{1,0:T(8,128)(2,1)S(1)} collective-permute-done((bf16[256,512]{1,0:T(8,128)(2,1)S(1)}, bf16[256,512]{1,0:T(8,128)(2,1)S(1)}, u32[]{:S(2)}, u32[]{:S(2)}) %collective-permute-start.22) | collective-permute-done | bytes 262176 | tf_op jit(solution)/shard_map/ppermute | solution.py:20
  113.0 1.4 pad_maximum_fusion
  116.9 3.4 %collective-permute-done.17 = f32[128,1792]{1,0:T(8,128)S(1)} collective-permute-done((f32[128,1792]{1,0:T(8,128)S(1)}, f32[128,1792]{1,0:T(8,128)S(1)}, u32[]{:S(2)}, u32[]{:S(2)}) %collective-permute-start.17) | collective-permute-done | bytes 917536 | tf_op jit(solution)/shard_map/ppermute | solution.py:24
  120.3 1.5 fusion
  121.8 3.5 %all-to-all-start.3 = ((bf16[4,32,1792]{2,1,0:T(8,128)(2,1)}), bf16[4,32,1792]{2,1,0:T(8,128)(2,1)S(1)}, u32[]{:S(2)}, u32[]{:S(2)}) async-start(bf16[4,32,1792]{2,1,0:T(8,128)(2,1)} %bitcast.6), calls=%async_computation.3 | async-start | bytes 917504 | tf_op jit(solution)/shard_map/all_to_all | solution.py:384
  125.3 3.5 %fusion.136 = (bf16[128,3584]{1,0:T(8,128)(2,1)S(1)}, f32[128,3584]{1,0:T(8,128)}) fusion(f32[128,3584]{1,0:T(8,128)} %collective-permute-done.24, f32[256,1792]{1,0:T(8,128)} %copy-done.4, f32[256,1792]{1,0:T(8,128)} %copy-done.5), kind=kLoop, calls=%fused_computation.372 | loop fusion | flops 1376256 | bytes 8257536 | tf_op jit(solution)/shard_map/convert.2
  129.5 2.0 collective-permute-start.27
  131.5 4.0 %collective-permute-start.26 = (bf16[32,3584]{1,0:T(8,128)(2,1)S(1)}, bf16[32,3584]{1,0:T(8,128)(2,1)S(1)}, u32[]{:S(2)}, u32[]{:S(2)}) collective-permute-start(bf16[32,3584]{1,0:T(8,128)(2,1)S(1)} %get-tuple-element.37), channel_id=1, source_target_pairs={{32,0},{48,16},{0,32},{16,48},{33,1},{49,17},{1,33},{17,49},{34,2}... | collective-permute-start | bytes 688136 | tf_op jit(solution)/shard_map/ppermute | solution.py:20
  135.5 5.7 %all-to-all-done.3 = bf16[4,32,1792]{2,1,0:T(8,128)(2,1)S(1)} async-done(((bf16[4,32,1792]{2,1,0:T(8,128)(2,1)}), bf16[4,32,1792]{2,1,0:T(8,128)(2,1)S(1)}, u32[]{:S(2)}, u32[]{:S(2)}) %all-to-all-start.3) | async-done | bytes 458784 | tf_op jit(solution)/shard_map/all_to_all | solution.py:384
  141.3 11.4 %collective-permute-done.25 = bf16[32,3584]{1,0:T(8,128)(2,1)S(1)} collective-permute-done((bf16[32,3584]{1,0:T(8,128)(2,1)}, bf16[32,3584]{1,0:T(8,128)(2,1)S(1)}, u32[]{:S(2)}, u32[]{:S(2)}) %collective-permute-start.25) | collective-permute-done | bytes 229408 | tf_op jit(solution)/shard_map/ppermute | solution.py:20
  152.8 2.7 %collective-permute-done.26 = bf16[32,3584]{1,0:T(8,128)(2,1)S(1)} collective-permute-done((bf16[32,3584]{1,0:T(8,128)(2,1)S(1)}, bf16[32,3584]{1,0:T(8,128)(2,1)S(1)}, u32[]{:S(2)}, u32[]{:S(2)}) %collective-permute-start.26) | collective-permute-done | bytes 229408 | tf_op jit(solution)/shard_map/ppermute | solution.py:20
  155.5 1.1 fusion.23
  157.6 4.3 %collective-permute-start.29 = (bf16[32,3584]{1,0:T(8,128)(2,1)S(1)}, bf16[32,3584]{1,0:T(8,128)(2,1)S(1)}, u32[]{:S(2)}, u32[]{:S(2)}) collective-permute-start(bf16[32,3584]{1,0:T(8,128)(2,1)S(1)} %pad_maximum_fusion.5), channel_id=1, source_target_pairs={{32,0},{48,16},{0,32},{16,48},{33,1},{49,17},{1,33},{17,49},{34,2}... | collective-permute-start | bytes 688136 | tf_op jit(solution)/shard_map/ppermute | solution.py:20
  162.3 3.7 %collective-permute-done.30 = bf16[32,3584]{1,0:T(8,128)(2,1)S(1)} collective-permute-done((bf16[32,3584]{1,0:T(8,128)(2,1)S(1)}, bf16[32,3584]{1,0:T(8,128)(2,1)S(1)}, u32[]{:S(2)}, u32[]{:S(2)}) %collective-permute-start.30) | collective-permute-done | bytes 229408 | tf_op jit(solution)/shard_map/ppermute | solution.py:20
  165.9 10.5 %collective-permute-done.29 = bf16[32,3584]{1,0:T(8,128)(2,1)S(1)} collective-permute-done((bf16[32,3584]{1,0:T(8,128)(2,1)S(1)}, bf16[32,3584]{1,0:T(8,128)(2,1)S(1)}, u32[]{:S(2)}, u32[]{:S(2)}) %collective-permute-start.29) | collective-permute-done | bytes 229408 | tf_op jit(solution)/shard_map/ppermute | solution.py:20
  176.5 4.1 %collective-permute-done.28 = bf16[32,3584]{1,0:T(8,128)(2,1)S(1)} collective-permute-done((bf16[32,3584]{1,0:T(8,128)(2,1)S(1)}, bf16[32,3584]{1,0:T(8,128)(2,1)S(1)}, u32[]{:S(2)}, u32[]{:S(2)}) %collective-permute-start.28) | collective-permute-done | bytes 229408 | tf_op jit(solution)/shard_map/ppermute | solution.py:20
  182.3 0.9 collective-permute-done.31
  184.9 1.5 collective-permute-start.34
  186.7 1.9 collective-permute-start.33
  188.9 1.5 collective-permute-start.32
  190.7 4.2 %collective-permute-done.34 = bf16[256,512]{1,0:T(8,128)(2,1)S(1)} collective-permute-done((bf16[256,512]{1,0:T(8,128)(2,1)S(1)}, bf16[256,512]{1,0:T(8,128)(2,1)S(1)}, u32[]{:S(2)}, u32[]{:S(2)}) %collective-permute-start.34) | collective-permute-done | bytes 262176 | tf_op jit(solution)/shard_map/ppermute | solution.py:20
  194.9 5.0 %collective-permute-done.33 = bf16[256,512]{1,0:T(8,128)(2,1)S(1)} collective-permute-done((bf16[256,512]{1,0:T(8,128)(2,1)S(1)}, bf16[256,512]{1,0:T(8,128)(2,1)S(1)}, u32[]{:S(2)}, u32[]{:S(2)}) %collective-permute-start.33) | collective-permute-done | bytes 262176 | tf_op jit(solution)/shard_map/ppermute | solution.py:20
  199.8 0.9 collective-permute-done.32
  201.9 2.8 %collective-permute-start.36 = (bf16[128,512]{1,0:T(8,128)(2,1)S(1)}, bf16[128,512]{1,0:T(8,128)(2,1)S(1)}, u32[]{:S(2)}, u32[]{:S(2)}) collective-permute-start(bf16[128,512]{1,0:T(8,128)(2,1)S(1)} %pad_maximum_fusion.8), channel_id=1, source_target_pairs={{1,0},{2,1},{3,2},{0,3},{5,4},{6,5},{7,6},{4,7},{9,8},{10,9},{11,1... | collective-permute-start | bytes 393224 | tf_op jit(solution)/shard_map/ppermute | solution.py:20
  204.8 4.3 %collective-permute-done.35 = bf16[128,512]{1,0:T(8,128)(2,1)S(1)} collective-permute-done((bf16[128,512]{1,0:T(8,128)(2,1)S(1)}, bf16[128,512]{1,0:T(8,128)(2,1)S(1)}, u32[]{:S(2)}, u32[]{:S(2)}) %collective-permute-start.35) | collective-permute-done | bytes 131104 | tf_op jit(solution)/shard_map/ppermute | solution.py:20
  209.5 1.4 collective-permute-done.37
  211.0 3.7 %collective-permute-start.38 = (bf16[2,32,512]{2,1,0:T(8,128)(2,1)S(1)}, bf16[2,32,512]{2,1,0:T(8,128)(2,1)S(1)}, u32[]{:S(2)}, u32[]{:S(2)}) collective-permute-start(bf16[2,32,512]{2,1,0:T(8,128)(2,1)S(1)} %fusion.63), channel_id=1, source_target_pairs={{0,4},{4,0},{1,5},{5,1},{2,6},{6,2},{3,7},{7,3},{8,12},{12,8},{9,1... | collective-permute-start | bytes 196616 | tf_op jit(solution)/shard_map/ppermute | solution.py:24
  215.4 3.9 %collective-permute-done.38 = bf16[2,32,512]{2,1,0:T(8,128)(2,1)S(1)} collective-permute-done((bf16[2,32,512]{2,1,0:T(8,128)(2,1)S(1)}, bf16[2,32,512]{2,1,0:T(8,128)(2,1)S(1)}, u32[]{:S(2)}, u32[]{:S(2)}) %collective-permute-start.38) | collective-permute-done | bytes 65568 | tf_op jit(solution)/shard_map/ppermute | solution.py:24
  (158 shorter events, 25.0 us)
Async XLA Ops:
  0.6 109.6 %copy-start = (bf16[512,1792]{1,0:T(8,128)(2,1)S(1)}, bf16[512,1792]{1,0:T(8,128)(2,1)}, u32[]{:S(2)}) copy-start(bf16[512,1792]{1,0:T(8,128)(2,1)} %param.25) | copy-start | bytes 5505028
  0.6 35.7 %copy-start.1 = (bf16[1600,128]{1,0:T(8,128)(2,1)S(1)}, bf16[1600,128]{1,0:T(8,128)(2,1)}, u32[]{:S(2)}) copy-start(bf16[1600,128]{1,0:T(8,128)(2,1)} %w0.1) | copy-start | bytes 1228804
  0.7 21.3 %copy-start.7 = (bf16[32,1600]{1,0:T(8,128)(2,1)S(1)}, bf16[32,1600]{1,0:T(8,128)(2,1)}, u32[]{:S(2)}) copy-start(bf16[32,1600]{1,0:T(8,128)(2,1)} %param.15) | copy-start | bytes 307204
  0.7 17.7 %copy-start.15 = (f32[1600]{0:T(1024)S(1)}, f32[1600]{0:T(1024)}, u32[]{:S(2)}) copy-start(f32[1600]{0:T(1024)} %param.16) | copy-start | bytes 19204
  0.7 17.7 %copy-start.16 = (f32[1600]{0:T(1024)S(1)}, f32[1600]{0:T(1024)}, u32[]{:S(2)}) copy-start(f32[1600]{0:T(1024)} %param.17) | copy-start | bytes 19204
  0.7 22.8 %copy-start.8 = (bf16[32,512]{1,0:T(8,128)(2,1)S(1)}, bf16[32,512]{1,0:T(8,128)(2,1)}, u32[]{:S(2)}) copy-start(bf16[32,512]{1,0:T(8,128)(2,1)} %param.22) | copy-start | bytes 98308
  0.7 22.8 %copy-start.9 = (bf16[32,512]{1,0:T(8,128)(2,1)S(1)}, bf16[32,512]{1,0:T(8,128)(2,1)}, u32[]{:S(2)}) copy-start(bf16[32,512]{1,0:T(8,128)(2,1)} %param.23) | copy-start | bytes 98308
  0.7 35.6 %collective-permute-start.5 = (bf16[1600,128]{1,0:T(8,128)(2,1)}, bf16[1600,128]{1,0:T(8,128)(2,1)S(1)}, u32[]{:S(2)}, u32[]{:S(2)}) collective-permute-start(bf16[1600,128]{1,0:T(8,128)(2,1)} %w0.1), channel_id=1, source_target_pairs={{128,0},{192,64},{0,128},{64,192},{129,1},{193,65},{1,129},{65,193... | collective-permute-start | bytes 1228808 | tf_op jit(solution)/shard_map/ppermute | solution.py:20
  4.0 32.3 %collective-permute-start.4 = (bf16[1600,128]{1,0:T(8,128)(2,1)}, bf16[1600,128]{1,0:T(8,128)(2,1)}, u32[]{:S(2)}, u32[]{:S(2)}) collective-permute-start(bf16[1600,128]{1,0:T(8,128)(2,1)} %w0.1), channel_id=1, source_target_pairs={{64,0},{128,64},{192,128},{0,192},{65,1},{129,65},{193,129},{1,193... | collective-permute-start | bytes 1228808 | tf_op jit(solution)/shard_map/ppermute | solution.py:20
  5.0 31.3 %collective-permute-start.6 = (bf16[1600,128]{1,0:T(8,128)(2,1)}, bf16[1600,128]{1,0:T(8,128)(2,1)}, u32[]{:S(2)}, u32[]{:S(2)}) collective-permute-start(bf16[1600,128]{1,0:T(8,128)(2,1)} %w0.1), channel_id=1, source_target_pairs={{192,0},{0,64},{64,128},{128,192},{193,1},{1,65},{65,129},{129,193... | collective-permute-start | bytes 1228808 | tf_op jit(solution)/shard_map/ppermute | solution.py:20
  6.0 15.9 %collective-permute-start = (bf16[32,1600]{1,0:T(8,128)(2,1)}, bf16[32,1600]{1,0:T(8,128)(2,1)S(1)}, u32[]{:S(2)}, u32[]{:S(2)}) collective-permute-start(bf16[32,1600]{1,0:T(8,128)(2,1)} %param.15), channel_id=1, source_target_pairs={{0,4},{4,0},{1,5},{5,1},{2,6},{6,2},{3,7},{7,3},{8,12},{12,8},{9,1... | collective-permute-start | bytes 307208 | tf_op jit(solution)/shard_map/ppermute | solution.py:24
  14.8 28.3 %all-to-all-start.1 = ((bf16[4,144,512]{2,1,0:T(8,128)(2,1)}), bf16[4,144,512]{2,1,0:T(8,128)(2,1)S(1)}, u32[]{:S(2)}, u32[]{:S(2)}) async-start(bf16[4,144,512]{2,1,0:T(8,128)(2,1)} %broadcast_in_dim.32), calls=%async_computation.1 | async-start | bytes 1179648 | tf_op jit(solution)/shard_map/all_to_all | solution.py:29
  20.5 1.4 copy-start.17
  22.0 8.4 %collective-permute-start.3 = (bf16[64,1600]{1,0:T(8,128)(2,1)S(1)}, bf16[64,1600]{1,0:T(8,128)(2,1)S(1)}, u32[]{:S(2)}, u32[]{:S(2)}) collective-permute-start(bf16[64,1600]{1,0:T(8,128)(2,1)S(1)} %maximum_select_fusion.x0), channel_id=1, source_target_pairs={{3,0},{0,1},{1,2},{2,3},{7,4},{4,5},{5,6},{6,7},{11,8},{8,9},{9,10... | collective-permute-start | bytes 614408 | tf_op jit(solution)/shard_map/ppermute | solution.py:20
  23.6 11.1 %collective-permute-start.2 = (bf16[64,1600]{1,0:T(8,128)(2,1)S(1)}, bf16[64,1600]{1,0:T(8,128)(2,1)S(1)}, u32[]{:S(2)}, u32[]{:S(2)}) collective-permute-start(bf16[64,1600]{1,0:T(8,128)(2,1)S(1)} %maximum_select_fusion.x0), channel_id=1, source_target_pairs={{2,0},{3,1},{0,2},{1,3},{6,4},{7,5},{4,6},{5,7},{10,8},{11,9},{8,1... | collective-permute-start | bytes 614408 | tf_op jit(solution)/shard_map/ppermute | solution.py:20
  30.4 5.9 %collective-permute-start.1 = (bf16[64,1600]{1,0:T(8,128)(2,1)S(1)}, bf16[64,1600]{1,0:T(8,128)(2,1)S(1)}, u32[]{:S(2)}, u32[]{:S(2)}) collective-permute-start(bf16[64,1600]{1,0:T(8,128)(2,1)S(1)} %maximum_select_fusion.x0), channel_id=1, source_target_pairs={{1,0},{2,1},{3,2},{0,3},{5,4},{6,5},{7,6},{4,7},{9,8},{10,9},{11,1... | collective-permute-start | bytes 614408 | tf_op jit(solution)/shard_map/ppermute | solution.py:20
  34.7 45.9 %collective-permute-start.13 = (bf16[32,1024]{1,0:T(8,128)(2,1)S(1)}, bf16[32,1024]{1,0:T(8,128)(2,1)S(1)}, u32[]{:S(2)}, u32[]{:S(2)}) collective-permute-start(bf16[32,1024]{1,0:T(8,128)(2,1)S(1)} %constant_dynamic-update-slice_fusion), channel_id=1, source_target_pairs={{0,4},{4,0},{1,5},{5,1},{2,6},{6,2},{3,7},{7,3},{8,12},{12,8},{9,1... | collective-permute-start | bytes 196616 | tf_op jit(solution)/shard_map/ppermute | solution.py:24
  40.3 1.8 collective-permute-start.7
  43.1 11.6 %all-to-all-start = ((bf16[4,80,384]{2,1,0:T(8,128)(2,1)}), bf16[4,80,384]{2,1,0:T(8,128)(2,1)S(1)}, u32[]{:S(2)}, u32[]{:S(2)}) async-start(bf16[4,80,384]{2,1,0:T(8,128)(2,1)} %pair_sum.1), calls=%async_computation | async-start | bytes 491520 | tf_op jit(solution)/shard_map/all_to_all | solution.py:327
  47.5 40.4 %copy-start.19 = (f32[512]{0:T(512)S(1)}, f32[512]{0:T(512)}, u32[]{:S(2)}) copy-start(f32[512]{0:T(512)} %param.21) | copy-start | bytes 6148
  56.1 10.3 %all-to-all-start.2 = ((bf16[4,64,256]{2,1,0:T(8,128)(2,1)}), bf16[4,64,256]{2,1,0:T(8,128)(2,1)S(1)}, u32[]{:S(2)}, u32[]{:S(2)}) async-start(bf16[4,64,256]{2,1,0:T(8,128)(2,1)} %broadcast_in_dim.35), calls=%async_computation.2 | async-start | bytes 262144 | tf_op jit(solution)/shard_map/all_to_all | solution.py:29
  66.4 1.3 collective-permute-start.8
  68.8 6.9 %collective-permute-start.9 = (bf16[64,512]{1,0:T(8,128)(2,1)S(1)}, bf16[64,512]{1,0:T(8,128)(2,1)S(1)}, u32[]{:S(2)}, u32[]{:S(2)}) collective-permute-start(bf16[64,512]{1,0:T(8,128)(2,1)S(1)} %get-tuple-element.12), channel_id=1, source_target_pairs={{1,0},{2,1},{3,2},{0,3},{5,4},{6,5},{7,6},{4,7},{9,8},{10,9},{11,1... | collective-permute-start | bytes 196616 | tf_op jit(solution)/shard_map/ppermute | solution.py:20
  72.6 6.1 %collective-permute-start.10 = (bf16[64,512]{1,0:T(8,128)(2,1)S(1)}, bf16[64,512]{1,0:T(8,128)(2,1)S(1)}, u32[]{:S(2)}, u32[]{:S(2)}) collective-permute-start(bf16[64,512]{1,0:T(8,128)(2,1)S(1)} %get-tuple-element.13), channel_id=1, source_target_pairs={{2,0},{3,1},{0,2},{1,3},{6,4},{7,5},{4,6},{5,7},{10,8},{11,9},{8,1... | collective-permute-start | bytes 196616 | tf_op jit(solution)/shard_map/ppermute | solution.py:20
  72.6 6.5 %collective-permute-start.11 = (bf16[64,512]{1,0:T(8,128)(2,1)S(1)}, bf16[64,512]{1,0:T(8,128)(2,1)S(1)}, u32[]{:S(2)}, u32[]{:S(2)}) collective-permute-start(bf16[64,512]{1,0:T(8,128)(2,1)S(1)} %get-tuple-element.14), channel_id=1, source_target_pairs={{3,0},{0,1},{1,2},{2,3},{7,4},{4,5},{5,6},{6,7},{11,8},{8,9},{9,10... | collective-permute-start | bytes 196616 | tf_op jit(solution)/shard_map/ppermute | solution.py:20
  79.1 8.8 %collective-permute-start.12 = (bf16[64,512]{1,0:T(8,128)(2,1)S(1)}, bf16[64,512]{1,0:T(8,128)(2,1)S(1)}, u32[]{:S(2)}, u32[]{:S(2)}) collective-permute-start(bf16[64,512]{1,0:T(8,128)(2,1)S(1)} %fusion.84), channel_id=1, source_target_pairs={{0,4},{4,0},{1,5},{5,1},{2,6},{6,2},{3,7},{7,3},{8,12},{12,8},{9,1... | collective-permute-start | bytes 196616 | tf_op jit(solution)/shard_map/ppermute | solution.py:24
  80.6 9.9 %collective-permute-start.16 = (bf16[64,1024]{1,0:T(8,128)(2,1)S(1)}, bf16[64,1024]{1,0:T(8,128)(2,1)S(1)}, u32[]{:S(2)}, u32[]{:S(2)}) collective-permute-start(bf16[64,1024]{1,0:T(8,128)(2,1)S(1)} %maximum_select_fusion.1), channel_id=1, source_target_pairs={{3,0},{0,1},{1,2},{2,3},{7,4},{4,5},{5,6},{6,7},{11,8},{8,9},{9,10... | collective-permute-start | bytes 393224 | tf_op jit(solution)/shard_map/ppermute | solution.py:20
  81.4 10.7 %collective-permute-start.15 = (bf16[64,1024]{1,0:T(8,128)(2,1)S(1)}, bf16[64,1024]{1,0:T(8,128)(2,1)S(1)}, u32[]{:S(2)}, u32[]{:S(2)}) collective-permute-start(bf16[64,1024]{1,0:T(8,128)(2,1)S(1)} %maximum_select_fusion.1), channel_id=1, source_target_pairs={{2,0},{3,1},{0,2},{1,3},{6,4},{7,5},{4,6},{5,7},{10,8},{11,9},{8,1... | collective-permute-start | bytes 393224 | tf_op jit(solution)/shard_map/ppermute | solution.py:20
  84.0 8.1 %collective-permute-start.14 = (bf16[64,1024]{1,0:T(8,128)(2,1)S(1)}, bf16[64,1024]{1,0:T(8,128)(2,1)S(1)}, u32[]{:S(2)}, u32[]{:S(2)}) collective-permute-start(bf16[64,1024]{1,0:T(8,128)(2,1)S(1)} %maximum_select_fusion.1), channel_id=1, source_target_pairs={{1,0},{2,1},{3,2},{0,3},{5,4},{6,5},{7,6},{4,7},{9,8},{10,9},{11,1... | collective-permute-start | bytes 393224 | tf_op jit(solution)/shard_map/ppermute | solution.py:20
  87.9 6.3 %collective-permute-start.20 = (bf16[64,512]{1,0:T(8,128)(2,1)S(1)}, bf16[64,512]{1,0:T(8,128)(2,1)S(1)}, u32[]{:S(2)}, u32[]{:S(2)}) collective-permute-start(bf16[64,512]{1,0:T(8,128)(2,1)S(1)} %get-tuple-element.32), channel_id=1, source_target_pairs={{3,0},{0,1},{1,2},{2,3},{7,4},{4,5},{5,6},{6,7},{11,8},{8,9},{9,10... | collective-permute-start | bytes 196616 | tf_op jit(solution)/shard_map/ppermute | solution.py:20
  88.0 6.2 %collective-permute-start.19 = (bf16[64,512]{1,0:T(8,128)(2,1)S(1)}, bf16[64,512]{1,0:T(8,128)(2,1)S(1)}, u32[]{:S(2)}, u32[]{:S(2)}) collective-permute-start(bf16[64,512]{1,0:T(8,128)(2,1)S(1)} %get-tuple-element.32), channel_id=1, source_target_pairs={{2,0},{3,1},{0,2},{1,3},{6,4},{7,5},{4,6},{5,7},{10,8},{11,9},{8,1... | collective-permute-start | bytes 196616 | tf_op jit(solution)/shard_map/ppermute | solution.py:20
  90.5 4.5 %collective-permute-start.18 = (bf16[64,512]{1,0:T(8,128)(2,1)S(1)}, bf16[64,512]{1,0:T(8,128)(2,1)S(1)}, u32[]{:S(2)}, u32[]{:S(2)}) collective-permute-start(bf16[64,512]{1,0:T(8,128)(2,1)S(1)} %get-tuple-element.32), channel_id=1, source_target_pairs={{1,0},{2,1},{3,2},{0,3},{5,4},{6,5},{7,6},{4,7},{9,8},{10,9},{11,1... | collective-permute-start | bytes 196616 | tf_op jit(solution)/shard_map/ppermute | solution.py:20
  95.0 10.0 %collective-permute-start.23 = (bf16[256,512]{1,0:T(8,128)(2,1)S(1)}, bf16[256,512]{1,0:T(8,128)(2,1)S(1)}, u32[]{:S(2)}, u32[]{:S(2)}) collective-permute-start(bf16[256,512]{1,0:T(8,128)(2,1)S(1)} %pad_maximum_fusion.3), channel_id=1, source_target_pairs={{192,0},{0,64},{64,128},{128,192},{193,1},{1,65},{65,129},{129,193... | collective-permute-start | bytes 786440 | tf_op jit(solution)/shard_map/ppermute | solution.py:20
  97.1 12.4 %collective-permute-start.22 = (bf16[256,512]{1,0:T(8,128)(2,1)S(1)}, bf16[256,512]{1,0:T(8,128)(2,1)S(1)}, u32[]{:S(2)}, u32[]{:S(2)}) collective-permute-start(bf16[256,512]{1,0:T(8,128)(2,1)S(1)} %pad_maximum_fusion.3), channel_id=1, source_target_pairs={{128,0},{192,64},{0,128},{64,192},{129,1},{193,65},{1,129},{65,193... | collective-permute-start | bytes 786440 | tf_op jit(solution)/shard_map/ppermute | solution.py:20
  99.8 9.7 %collective-permute-start.21 = (bf16[256,512]{1,0:T(8,128)(2,1)S(1)}, bf16[256,512]{1,0:T(8,128)(2,1)S(1)}, u32[]{:S(2)}, u32[]{:S(2)}) collective-permute-start(bf16[256,512]{1,0:T(8,128)(2,1)S(1)} %pad_maximum_fusion.3), channel_id=1, source_target_pairs={{64,0},{128,64},{192,128},{0,192},{65,1},{129,65},{193,129},{1,193... | collective-permute-start | bytes 786440 | tf_op jit(solution)/shard_map/ppermute | solution.py:20
  110.3 1.5 copy-start.2
  111.8 1.3 copy-start.4
  113.0 1.9 copy-start.5
  113.0 2.8 %copy-start.6 = (bf16[1792,512]{1,0:T(8,128)(2,1)S(1)}, bf16[1792,512]{1,0:T(8,128)(2,1)}, u32[]{:S(2)}) copy-start(bf16[1792,512]{1,0:T(8,128)(2,1)} %param.26) | copy-start | bytes 5505028
  114.9 1.8 copy-start.14
  114.9 1.8 copy-start.18
  114.9 1.9 copy-start.13
  114.9 1.9 copy-start.12
  114.9 10.4 %collective-permute-start.24 = (f32[128,3584]{1,0:T(8,128)}, f32[128,3584]{1,0:T(8,128)}, u32[]{:S(2)}, u32[]{:S(2)}) collective-permute-start(f32[128,3584]{1,0:T(8,128)} %pad_maximum_fusion), channel_id=1, source_target_pairs={{0,8},{8,0},{1,9},{9,1},{2,10},{10,2},{3,11},{11,3},{4,12},{12,4},... | collective-permute-start | bytes 5505032 | tf_op jit(solution)/shard_map/ppermute | solution.py:24
  116.6 3.7 %collective-permute-start.17 = (f32[128,1792]{1,0:T(8,128)S(1)}, f32[128,1792]{1,0:T(8,128)S(1)}, u32[]{:S(2)}, u32[]{:S(2)}) collective-permute-start(f32[128,1792]{1,0:T(8,128)S(1)} %fusion.42), channel_id=1, source_target_pairs={{0,8},{8,0},{1,9},{9,1},{2,10},{10,2},{3,11},{11,3},{4,12},{12,4},... | collective-permute-start | bytes 2752520 | tf_op jit(solution)/shard_map/ppermute | solution.py:24
  121.8 19.4 %all-to-all-start.3 = ((bf16[4,32,1792]{2,1,0:T(8,128)(2,1)}), bf16[4,32,1792]{2,1,0:T(8,128)(2,1)S(1)}, u32[]{:S(2)}, u32[]{:S(2)}) async-start(bf16[4,32,1792]{2,1,0:T(8,128)(2,1)} %bitcast.6), calls=%async_computation.3 | async-start | bytes 917504 | tf_op jit(solution)/shard_map/all_to_all | solution.py:384
  125.3 10.3 %copy-start.11 = (s32[256]{0:T(256)S(1)}, s32[256]{0:T(256)}, u32[]{:S(2)}) copy-start(s32[256]{0:T(256)} %get-tuple-element.22) | copy-start | bytes 3076
  129.5 23.2 %collective-permute-start.25 = (bf16[32,3584]{1,0:T(8,128)(2,1)}, bf16[32,3584]{1,0:T(8,128)(2,1)S(1)}, u32[]{:S(2)}, u32[]{:S(2)}) collective-permute-start(bf16[32,3584]{1,0:T(8,128)(2,1)} %get-tuple-element.35), channel_id=1, source_target_pairs={{16,0},{32,16},{48,32},{0,48},{17,1},{33,17},{49,33},{1,49},{18,2}... | collective-permute-start | bytes 688136 | tf_op jit(solution)/shard_map/ppermute | solution.py:20
  129.5 23.2 %collective-permute-start.27 = (bf16[32,3584]{1,0:T(8,128)(2,1)S(1)}, bf16[32,3584]{1,0:T(8,128)(2,1)S(1)}, u32[]{:S(2)}, u32[]{:S(2)}) collective-permute-start(bf16[32,3584]{1,0:T(8,128)(2,1)S(1)} %get-tuple-element.36), channel_id=1, source_target_pairs={{48,0},{0,16},{16,32},{32,48},{49,1},{1,17},{17,33},{33,49},{50,2}... | collective-permute-start | bytes 688136 | tf_op jit(solution)/shard_map/ppermute | solution.py:20
  131.5 23.9 %collective-permute-start.26 = (bf16[32,3584]{1,0:T(8,128)(2,1)S(1)}, bf16[32,3584]{1,0:T(8,128)(2,1)S(1)}, u32[]{:S(2)}, u32[]{:S(2)}) collective-permute-start(bf16[32,3584]{1,0:T(8,128)(2,1)S(1)} %get-tuple-element.37), channel_id=1, source_target_pairs={{32,0},{48,16},{0,32},{16,48},{33,1},{49,17},{1,33},{17,49},{34,2}... | collective-permute-start | bytes 688136 | tf_op jit(solution)/shard_map/ppermute | solution.py:20
  135.5 26.7 %copy-start.10 = (s32[256]{0:T(256)S(1)}, s32[256]{0:T(256)}, u32[]{:S(2)}) copy-start(s32[256]{0:T(256)} %get-tuple-element.23) | copy-start | bytes 3076
  156.7 9.2 %collective-permute-start.30 = (bf16[32,3584]{1,0:T(8,128)(2,1)S(1)}, bf16[32,3584]{1,0:T(8,128)(2,1)S(1)}, u32[]{:S(2)}, u32[]{:S(2)}) collective-permute-start(bf16[32,3584]{1,0:T(8,128)(2,1)S(1)} %pad_maximum_fusion.5), channel_id=1, source_target_pairs={{48,0},{0,16},{16,32},{32,48},{49,1},{1,17},{17,33},{33,49},{50,2}... | collective-permute-start | bytes 688136 | tf_op jit(solution)/shard_map/ppermute | solution.py:20
  157.6 18.9 %collective-permute-start.29 = (bf16[32,3584]{1,0:T(8,128)(2,1)S(1)}, bf16[32,3584]{1,0:T(8,128)(2,1)S(1)}, u32[]{:S(2)}, u32[]{:S(2)}) collective-permute-start(bf16[32,3584]{1,0:T(8,128)(2,1)S(1)} %pad_maximum_fusion.5), channel_id=1, source_target_pairs={{32,0},{48,16},{0,32},{16,48},{33,1},{49,17},{1,33},{17,49},{34,2}... | collective-permute-start | bytes 688136 | tf_op jit(solution)/shard_map/ppermute | solution.py:20
  161.8 18.7 %collective-permute-start.28 = (bf16[32,3584]{1,0:T(8,128)(2,1)S(1)}, bf16[32,3584]{1,0:T(8,128)(2,1)S(1)}, u32[]{:S(2)}, u32[]{:S(2)}) collective-permute-start(bf16[32,3584]{1,0:T(8,128)(2,1)S(1)} %pad_maximum_fusion.5), channel_id=1, source_target_pairs={{16,0},{32,16},{48,32},{0,48},{17,1},{33,17},{49,33},{1,49},{18,2}... | collective-permute-start | bytes 688136 | tf_op jit(solution)/shard_map/ppermute | solution.py:20
  162.2 19.3 %copy-start.3 = (bf16[512,1792]{1,0:T(8,128)(2,1)S(1)}, bf16[512,1792]{1,0:T(8,128)(2,1)}, u32[]{:S(2)}) copy-start(bf16[512,1792]{1,0:T(8,128)(2,1)} %param.24) | copy-start | bytes 5505028
  180.6 2.6 %collective-permute-start.31 = (bf16[128,3584]{1,0:T(8,128)(2,1)S(1)}, bf16[128,3584]{1,0:T(8,128)(2,1)S(1)}, u32[]{:S(2)}, u32[]{:S(2)}) collective-permute-start(bf16[128,3584]{1,0:T(8,128)(2,1)S(1)} %pad_maximum_fusion.1), channel_id=1, source_target_pairs={{0,8},{8,0},{1,9},{9,1},{2,10},{10,2},{3,11},{11,3},{4,12},{12,4},... | collective-permute-start | bytes 2752520 | tf_op jit(solution)/shard_map/ppermute | solution.py:24
  184.9 9.9 %collective-permute-start.34 = (bf16[256,512]{1,0:T(8,128)(2,1)S(1)}, bf16[256,512]{1,0:T(8,128)(2,1)S(1)}, u32[]{:S(2)}, u32[]{:S(2)}) collective-permute-start(bf16[256,512]{1,0:T(8,128)(2,1)S(1)} %convolution_convert_fusion), channel_id=1, source_target_pairs={{192,0},{0,64},{64,128},{128,192},{193,1},{1,65},{65,129},{129,193... | collective-permute-start | bytes 786440 | tf_op jit(solution)/shard_map/ppermute | solution.py:20
  186.7 13.2 %collective-permute-start.33 = (bf16[256,512]{1,0:T(8,128)(2,1)S(1)}, bf16[256,512]{1,0:T(8,128)(2,1)S(1)}, u32[]{:S(2)}, u32[]{:S(2)}) collective-permute-start(bf16[256,512]{1,0:T(8,128)(2,1)S(1)} %convolution_convert_fusion.1), channel_id=1, source_target_pairs={{64,0},{128,64},{192,128},{0,192},{65,1},{129,65},{193,129},{1,193... | collective-permute-start | bytes 786440 | tf_op jit(solution)/shard_map/ppermute | solution.py:20
  188.9 11.8 %collective-permute-start.32 = (bf16[256,512]{1,0:T(8,128)(2,1)S(1)}, bf16[256,512]{1,0:T(8,128)(2,1)S(1)}, u32[]{:S(2)}, u32[]{:S(2)}) collective-permute-start(bf16[256,512]{1,0:T(8,128)(2,1)S(1)} %convolution_convert_fusion.2), channel_id=1, source_target_pairs={{128,0},{192,64},{0,128},{64,192},{129,1},{193,65},{1,129},{65,193... | collective-permute-start | bytes 786440 | tf_op jit(solution)/shard_map/ppermute | solution.py:20
  201.0 8.0 %collective-permute-start.35 = (bf16[128,512]{1,0:T(8,128)(2,1)S(1)}, bf16[128,512]{1,0:T(8,128)(2,1)S(1)}, u32[]{:S(2)}, u32[]{:S(2)}) collective-permute-start(bf16[128,512]{1,0:T(8,128)(2,1)S(1)} %pad_maximum_fusion.7), channel_id=1, source_target_pairs={{2,0},{3,1},{0,2},{1,3},{6,4},{7,5},{4,6},{5,7},{10,8},{11,9},{8,1... | collective-permute-start | bytes 393224 | tf_op jit(solution)/shard_map/ppermute | solution.py:20
  201.9 7.7 %collective-permute-start.36 = (bf16[128,512]{1,0:T(8,128)(2,1)S(1)}, bf16[128,512]{1,0:T(8,128)(2,1)S(1)}, u32[]{:S(2)}, u32[]{:S(2)}) collective-permute-start(bf16[128,512]{1,0:T(8,128)(2,1)S(1)} %pad_maximum_fusion.8), channel_id=1, source_target_pairs={{1,0},{2,1},{3,2},{0,3},{5,4},{6,5},{7,6},{4,7},{9,8},{10,9},{11,1... | collective-permute-start | bytes 393224 | tf_op jit(solution)/shard_map/ppermute | solution.py:20
  204.7 6.3 %collective-permute-start.37 = (bf16[128,512]{1,0:T(8,128)(2,1)S(1)}, bf16[128,512]{1,0:T(8,128)(2,1)S(1)}, u32[]{:S(2)}, u32[]{:S(2)}) collective-permute-start(bf16[128,512]{1,0:T(8,128)(2,1)S(1)} %pad_maximum_fusion.9), channel_id=1, source_target_pairs={{3,0},{0,1},{1,2},{2,3},{7,4},{4,5},{5,6},{6,7},{11,8},{8,9},{9,10... | collective-permute-start | bytes 393224 | tf_op jit(solution)/shard_map/ppermute | solution.py:20
  211.0 8.3 %collective-permute-start.38 = (bf16[2,32,512]{2,1,0:T(8,128)(2,1)S(1)}, bf16[2,32,512]{2,1,0:T(8,128)(2,1)S(1)}, u32[]{:S(2)}, u32[]{:S(2)}) collective-permute-start(bf16[2,32,512]{2,1,0:T(8,128)(2,1)S(1)} %fusion.63), channel_id=1, source_target_pairs={{0,4},{4,0},{1,5},{5,1},{2,6},{6,2},{3,7},{7,3},{8,12},{12,8},{9,1... | collective-permute-start | bytes 196616 | tf_op jit(solution)/shard_map/ppermute | solution.py:24
